TPU v7x, 32 devices: a whole 2x2x4 slice. The times are simulated.
32 devices in a mesh: tm: 8 (over y, x, core), batch: 4 (over z).
Axes of the slice: x: 2, y: 2, z: 4, core: 2. Of those that a mesh axis runs over, the one named last changes fastest.
Arguments:
- hidden_states: bfloat16 [4, 1024, 5120], P('batch', 'tm'), may hold values from -6 to 6
- gen_weight: bfloat16 [64, 5120], replicated, may hold values from -0.078125 to 0.078125
- noise_field: bfloat16 [4, 64, 1024], P('batch', None, 'tm'), may hold values from -6 to 6
- timesteps: int32 [4], P('batch'), may hold values from 200 to 999
- embed_real: bfloat16 [128, 5120], replicated, may hold values from -0.5 to 0.5
- time_real: bfloat16 [256, 3, 5120], P('tm'), may hold values from -0.375 to 0.375
- query_real: bfloat16 [5120, 1024], P(None, 'tm'), may hold values from -3 to 3
- key_real: bfloat16 [5120, 1024], P(None, 'tm'), may hold values from -3 to 3
- value_real: bfloat16 [5120, 1024], P(None, 'tm'), may hold values from -0.078125 to 0.078125
- out_real: bfloat16 [1024, 5120], P('tm'), may hold values from -0.1875 to 0.1875
- gain_real: float32 [2, 1024], P(None, 'tm'), may hold values from 0.25 to 3
- proj_real: bfloat16 [64, 5120], replicated, may hold values from -0.078125 to 0.078125
- embed_fake: bfloat16 [128, 5120], replicated, may hold values from -0.5 to 0.5
- time_fake: bfloat16 [256, 3, 5120], P('tm'), may hold values from -0.375 to 0.375
- query_fake: bfloat16 [5120, 1024], P(None, 'tm'), may hold values from -3 to 3
- key_fake: bfloat16 [5120, 1024], P(None, 'tm'), may hold values from -3 to 3
- value_fake: bfloat16 [5120, 1024], P(None, 'tm'), may hold values from -0.078125 to 0.078125
- out_fake: bfloat16 [1024, 5120], P('tm'), may hold values from -0.1875 to 0.1875
- gain_fake: float32 [2, 1024], P(None, 'tm'), may hold values from 0.25 to 3
- proj_fake: bfloat16 [64, 5120], replicated, may hold values from -0.078125 to 0.078125
Outputs:
- dmd_gradient: float32 [4, 64, 1024], P('batch', None, 'tm')
- weight_grad: float32 [64, 5120], replicated
All inputs are finite; a program needn't handle non-finite values.
Results may differ from a plain program's by a relative error of at most 0.019.
Values may be sent and summed in bfloat16 or wider, within the bound.
A program may use at most 128 MiB of HBM per device.

v0:
```python
import math

import jax
import jax.numpy as jnp
from jax import lax
from jax.sharding import PartitionSpec as P

HD = 128
FREQ = 256
FTOK = 128


norm_floor = 0.05
gap_floor = 0.25
highest = lax.Precision.HIGHEST


def from_behind(shard, axis, by):
    size = lax.axis_size(axis)
    pairs = [(i, i + by) for i in range(size) if 0 <= i + by < size]
    return lax.ppermute(shard, axis, pairs)


def sinusoid(time_step):
    half_freq = FREQ // 2
    frequency = jnp.exp(-math.log(10000.0) * jnp.arange(half_freq, dtype=jnp.float32) / half_freq)
    angles = time_step.astype(jnp.float32) * frequency
    return jnp.concatenate([jnp.cos(angles), jnp.sin(angles)]).astype(jnp.bfloat16)


def embed_stats(stacked, embed_table):
    embedded = lax.dot_general(
        stacked, embed_table, (((0,), (0,)), ((), ())), preferred_element_type=jnp.float32
    )
    row_mean = jnp.mean(embedded, axis=1)
    centered = embedded - row_mean[:, None]
    rscale = lax.rsqrt(jnp.mean(centered * centered, axis=1) + norm_floor)
    return (embedded, row_mean, rscale)


def fold_heads(embed_table, modulation, query_proj, key_proj, value_proj):
    scale_row = 1.0 + modulation[1]
    widened = embed_table.astype(jnp.float32) * scale_row[None, :]

    def fold_one(weight):
        wide_weight = weight.astype(jnp.float32)
        main_part = jnp.dot(widened, wide_weight, precision=highest)
        column_sum = jnp.dot(scale_row, wide_weight, precision=highest)
        offset = jnp.dot(modulation[0], wide_weight, precision=highest)
        return jnp.concatenate([main_part, column_sum[None, :], offset[None, :]], axis=0)

    return jnp.stack([fold_one(query_proj), fold_one(key_proj), fold_one(value_proj)])


def project(stacked, row_mean, rscale, folded):
    kin_rows = stacked.shape[0]
    base_part = jnp.einsum(
        "kr,pkc->prc", stacked.astype(jnp.float32), folded[:, :kin_rows], precision=highest
    )
    return (
        rscale[None, :, None] * base_part
        - (rscale * row_mean)[None, :, None] * folded[:, kin_rows][:, None, :]
        + folded[:, kin_rows + 1][:, None, :]
    )


def rms_round(vector, total_sq, columns, gain_row):
    return (
        vector * lax.rsqrt(total_sq / columns + norm_floor)[:, None] * gain_row[None, :]
    ).astype(jnp.bfloat16)


def attend(query_norm, key_norm, value_norm):
    token_count = query_norm.shape[0]
    block_rows = min(512, token_count)
    frames = jnp.arange(token_count, dtype=jnp.int32) // FTOK

    def one_block(row_start):
        query_block = lax.dynamic_slice_in_dim(query_norm, row_start, block_rows, 0)
        scores = jnp.einsum(
            "qhd,khd->hqk", query_block, key_norm, preferred_element_type=jnp.float32
        ) / math.sqrt(HD)
        query_frames = lax.dynamic_slice_in_dim(frames, row_start, block_rows, 0)
        allowed = frames[None, :] <= query_frames[:, None]
        scores = jnp.where(allowed[None], scores, -1e30)
        row_peak = jnp.max(scores, axis=2, keepdims=True)
        exp_scores = jnp.exp(scores - row_peak)
        attn_probs = (exp_scores / jnp.sum(exp_scores, axis=2, keepdims=True)).astype(jnp.bfloat16)
        return jnp.einsum(
            "hqk,khd->qhd", attn_probs, value_norm, preferred_element_type=jnp.float32
        ).astype(jnp.bfloat16)

    starts = jnp.arange(token_count // block_rows, dtype=jnp.int32) * block_rows
    pieces = lax.map(one_block, starts)
    return pieces.reshape(token_count, query_norm.shape[1], query_norm.shape[2])


def head_terms(attended, out_rows, modulation, final_proj):
    gated = out_rows.astype(jnp.float32) * modulation[2][None, :]
    folded_out = lax.dot_general(
        gated, final_proj.astype(jnp.float32), (((1,), (1,)), ((), ())), precision=highest
    )
    flat_heads = attended.reshape(attended.shape[0], -1).astype(jnp.float32)
    return lax.dot_general(folded_out, flat_heads, (((0,), (1,)), ((), ())), precision=highest)


def per_device(
    hidden_states,
    gen_weight,
    noise_field,
    timesteps,
    embed_real,
    time_real,
    query_real,
    key_real,
    value_real,
    out_real,
    gain_real,
    proj_real,
    embed_fake,
    time_fake,
    query_fake,
    key_fake,
    value_fake,
    out_fake,
    gain_fake,
    proj_fake,
):
    devices = lax.axis_size("tm")
    frame_tokens = hidden_states.shape[1]
    tokens = frame_tokens * devices
    patch_rows = gen_weight.shape[0]
    time_step = timesteps[0]
    level_raw = time_step.astype(jnp.float32) / 1000.0
    noise_level = 5.0 * level_raw / (1.0 + 4.0 * level_raw)
    generated = lax.dot_general(
        gen_weight, hidden_states[0], (((1,), (1,)), ((), ())), preferred_element_type=jnp.float32
    ).astype(jnp.bfloat16)
    noisy_patch = (
        (1.0 - noise_level) * generated.astype(jnp.float32)
        + noise_level * noise_field[0].astype(jnp.float32)
    ).astype(jnp.bfloat16)
    sinus_wave = sinusoid(time_step)
    freq_rows = time_real.shape[0]
    own_wave = lax.dynamic_slice_in_dim(sinus_wave, lax.axis_index("tm") * freq_rows, freq_rows, 0)
    share_real = jnp.einsum("f,fcd->cd", own_wave, time_real, preferred_element_type=jnp.float32)
    share_fake = jnp.einsum("f,fcd->cd", own_wave, time_fake, preferred_element_type=jnp.float32)
    modul_real, modul_fake = lax.psum((share_real, share_fake), "tm")
    earlier = from_behind(noisy_patch, "tm", 1)
    stacked = jnp.concatenate([noisy_patch, earlier], axis=0)
    embedded_real, mean_real, rscale_real = embed_stats(stacked, embed_real)
    embedded_fake, mean_fake, rscale_fake = embed_stats(stacked, embed_fake)
    folded_real = fold_heads(embed_real, modul_real, query_real, key_real, value_real)
    folded_fake = fold_heads(embed_fake, modul_fake, query_fake, key_fake, value_fake)
    local_width = query_real.shape[1]
    local_heads = local_width // HD
    columns = local_width * devices
    gathered = (
        lax.all_gather(noisy_patch.astype(jnp.float32), "tm", axis=1, tiled=True),
        lax.all_gather(mean_real, "tm", axis=0, tiled=True),
        lax.all_gather(rscale_real, "tm", axis=0, tiled=True),
        lax.all_gather(mean_fake, "tm", axis=0, tiled=True),
        lax.all_gather(rscale_fake, "tm", axis=0, tiled=True),
    )
    all_patch = gathered[0].astype(jnp.bfloat16)
    prior_frame = jnp.concatenate(
        [
            jnp.zeros((patch_rows, frame_tokens), jnp.bfloat16),
            all_patch[:, : tokens - frame_tokens],
        ],
        axis=1,
    )
    all_stacked = jnp.concatenate([all_patch, prior_frame], axis=0)
    qkv_real = project(all_stacked, gathered[1], gathered[2], folded_real)
    qkv_fake = project(all_stacked, gathered[3], gathered[4], folded_fake)
    norm_sums = lax.psum(
        (
            jnp.sum(qkv_real[0] * qkv_real[0], axis=1),
            jnp.sum(qkv_real[1] * qkv_real[1], axis=1),
            jnp.sum(qkv_fake[0] * qkv_fake[0], axis=1),
            jnp.sum(qkv_fake[1] * qkv_fake[1], axis=1),
        ),
        "tm",
    )
    head_shape = (tokens, local_heads, HD)
    attended_real = attend(
        rms_round(qkv_real[0], norm_sums[0], columns, gain_real[0]).reshape(head_shape),
        rms_round(qkv_real[1], norm_sums[1], columns, gain_real[1]).reshape(head_shape),
        qkv_real[2].astype(jnp.bfloat16).reshape(head_shape),
    )
    attended_fake = attend(
        rms_round(qkv_fake[0], norm_sums[2], columns, gain_fake[0]).reshape(head_shape),
        rms_round(qkv_fake[1], norm_sums[3], columns, gain_fake[1]).reshape(head_shape),
        qkv_fake[2].astype(jnp.bfloat16).reshape(head_shape),
    )
    term_real = head_terms(attended_real, out_real, modul_real, proj_real)
    term_fake = head_terms(attended_fake, out_fake, modul_fake, proj_fake)
    own_real, own_fake = (
        lax.psum_scatter(term_real, "tm", scatter_dimension=1, tiled=True),
        lax.psum_scatter(term_fake, "tm", scatter_dimension=1, tiled=True),
    )
    velocity_real = own_real + lax.dot_general(
        proj_real.astype(jnp.float32), embedded_real, (((1,), (1,)), ((), ())), precision=highest
    )
    velocity_fake = own_fake + lax.dot_general(
        proj_fake.astype(jnp.float32), embedded_fake, (((1,), (1,)), ((), ())), precision=highest
    )
    pred_real = noisy_patch.astype(jnp.float32) - noise_level * velocity_real
    pred_fake = noisy_patch.astype(jnp.float32) - noise_level * velocity_fake
    gap_local = jnp.sum(jnp.abs(generated.astype(jnp.float32) - pred_real))
    count_all = patch_rows * tokens
    grad_root = math.sqrt(lax.axis_size("batch") * hidden_states.shape[0] * tokens)
    gap_diff = pred_fake - pred_real
    difference = gap_diff.astype(jnp.bfloat16)
    partial_grad = jnp.dot(difference, hidden_states[0], preferred_element_type=jnp.float32)
    gap_total = lax.psum(gap_local, "tm")
    normalizer = jnp.maximum(gap_total / count_all, gap_floor)
    weight_grad = lax.psum(partial_grad / normalizer / grad_root, ("tm", "batch"))
    dmd_gradient = (gap_diff / normalizer)[None]
    return (dmd_gradient, weight_grad)


def solution(mesh):
    in_specs = (
        P("batch", "tm", None),
        P(),
        P("batch", None, "tm"),
        P("batch"),
        P(),
        P("tm", None, None),
        P(None, "tm"),
        P(None, "tm"),
        P(None, "tm"),
        P("tm", None),
        P(None, "tm"),
        P(),
        P(),
        P("tm", None, None),
        P(None, "tm"),
        P(None, "tm"),
        P(None, "tm"),
        P("tm", None),
        P(None, "tm"),
        P(),
    )
    out_specs = (P("batch", None, "tm"), P())
    return jax.shard_map(
        per_device, mesh=mesh, in_specs=in_specs, out_specs=out_specs, check_vma=False
    )
```

profile of v0, /device:TPU:1, one launch (start us, length us, event | category | flops | bytes accessed | tf_op | source)
XLA Modules:
  0.0 417.8 jit_solution(4317178082355693844)
XLA Ops:
  8.5 2.4 fusion.74
  10.9 4.5 %collective-permute-start = (bf16[64,128]{1,0:T(8,128)(2,1)S(1)}, bf16[64,128]{1,0:T(8,128)(2,1)S(1)}, u32[]{:S(2)}, u32[]{:S(2)}) collective-permute-start(bf16[64,128]{1,0:T(8,128)(2,1)S(1)} %get-tuple-element.224), channel_id=1, source_target_pairs={{0,4},{4,8},{8,12},{12,16},{16,20},{20,24},{24,28},{1,5},{5,9},{9,... | collective-permute-start | bytes 49160 | tf_op jit(solution)/shard_map/ppermute | solution.py:21
  16.5 1.5 fusion.99
  18.1 21.3 %psum.59 = f32[3,5120]{1,0:T(4,128)S(1)} all-reduce(f32[3,5120]{1,0:T(4,128)S(1)} %bitcast.296), channel_id=1, replica_groups=mesh['tm'=8,'batch'=4] {'tm'}, use_global_device_ids=true, to_apply=%region_12.0 | all-reduce | flops 15360 | bytes 122880 | tf_op jit(solution)/shard_map/psum | solution.py:148
  42.4 1.5 fusion.17
  44.0 1.5 fusion.18
  46.7 1.5 fusion.19
  49.0 1.3 slice_bitcast_fusion.8
  50.4 1.5 fusion.101
  52.5 3.7 fusion.20
  56.2 12.4 %all_gather.16 = bf16[64,1024]{1,0:T(8,128)(2,1)S(1)} all-gather(bf16[64,128]{1,0:T(8,128)(2,1)S(1)} %get-tuple-element.224), channel_id=1, replica_groups=mesh['tm'=8,'batch'=4] {'tm'}, dimensions={1}, use_global_device_ids=true | all-gather | bytes 147456 | tf_op jit(solution)/shard_map/all_gather | solution.py:159
  70.4 7.6 %all-gather.2 = f32[8,1,128]{2,1,0:T(1,128)S(1)} all-gather(f32[1,1,128]{2,1,0:T(1,128)S(1)} %rsqrt_bitcast_fusion), channel_id=1, replica_groups=mesh['tm'=8,'batch'=4] {'tm'}, dimensions={0}, use_global_device_ids=true | all-gather | bytes 4608 | tf_op jit(solution)/shard_map/all_gather | solution.py:161
  78.0 9.0 %all-gather.3 = f32[8,1,128]{2,1,0:T(1,128)S(1)} all-gather(f32[1,1,128]{2,1,0:T(1,128)S(1)} %get-tuple-element.222), channel_id=1, replica_groups=mesh['tm'=8,'batch'=4] {'tm'}, dimensions={0}, use_global_device_ids=true | all-gather | bytes 4608 | tf_op jit(solution)/shard_map/all_gather | solution.py:160
  87.0 1.0 fusion.29
  88.0 0.8 multiply_reduce_fusion.2
  90.4 0.9 copy-done.1
  91.4 0.9 multiply_reduce_fusion.1
  92.4 1.2 rsqrt_bitcast_fusion.1
  93.6 0.8 copy.45
  94.4 7.9 %all-gather = f32[8,1,128]{2,1,0:T(1,128)S(1)} all-gather(f32[1,1,128]{2,1,0:T(1,128)} %rsqrt_bitcast_fusion.1), channel_id=1, replica_groups=mesh['tm'=8,'batch'=4] {'tm'}, dimensions={0}, use_global_device_ids=true | all-gather | bytes 4608 | tf_op jit(solution)/shard_map/all_gather | solution.py:163
  102.3 8.7 %all-gather.1 = f32[8,1,128]{2,1,0:T(1,128)S(1)} all-gather(f32[1,1,128]{2,1,0:T(1,128)} %get-tuple-element.220), channel_id=1, replica_groups=mesh['tm'=8,'batch'=4] {'tm'}, dimensions={0}, use_global_device_ids=true | all-gather | bytes 4608 | tf_op jit(solution)/shard_map/all_gather | solution.py:162
  111.5 33.2 %all-reduce.8.cloned.1.call-done = (f32[1024]{0:T(1024)}, f32[1024]{0:T(1024)}, f32[3,5120]{1,0:T(4,128)}) async-done(((f32[1024]{0:T(1024)}, f32[1024]{0:T(1024)}, f32[3,5120]{1,0:T(4,128)}), (f32[1024]{0:T(1024)}, f32[1024]{0:T(1024)}, f32[3,5120]{1,0:T(4,128)})) %all-reduce.8.cloned.1.call-update) | async-done | bytes 69648 | tf_op jit(solution)/shard_map/psum | solution.py:176
  144.8 1.7 slice_add_fusion.1
  146.5 2.0 fusion.93
  148.4 2.0 fusion.83
  151.8 1.5 fusion.23
  153.3 1.5 fusion.24
  156.1 1.5 fusion.25
  158.9 9.1 %while.23 = (s32[]{:T(128)}, bf16[2,512,1,128]{3,1,2,0:T(8,128)(2,1)S(1)}, s32[1024]{0:T(1024)S(1)}, s32[2]{0:T(128)S(1)}, bf16[1024,1,128]{0,2,1:T(8,128)(2,1)S...) while((s32[]{:T(128)}, ...), condition=%wide.region_22.23_spmd.clone, body=%wide.region_19.22_spmd.clone.sunk | while | flops 273218560 | bytes 7098535 | solution.py:94
  168.0 1.1 fusion.120
  169.4 2.1 fusion.30
  172.2 1.8 copy.41
  174.7 3.9 fusion.26
  178.6 23.9 %reduce-scatter.5.cloned.1.call-done = f32[64,128]{1,0:T(8,128)} async-done(((f32[64,1024]{1,0:T(8,128)}), f32[64,128]{1,0:T(8,128)}) %reduce-scatter.5.cloned.1.call-update) | async-done | bytes 32784 | tf_op jit(solution)/shard_map/reduce_scatter | solution.py:199
  202.4 4.6 %abs_reduce_fusion = (f32[]{:T(128)}, f32[64,128]{1,0:T(8,128)}) fusion(f32[64,128]{1,0:T(8,128)} %get-tuple-element.225, f32[64,128]{1,0:T(8,128)} %reduce-scatter.5.cloned.1.call-done, f32[128,5120]{1,0:T(8,128)} %copy-done.2, bf16[64,5120]{1,0:T(8,128)(2,1)S(1)} %copy-done.15, f32[]{:T(128)S(6)} %div.95, bf16[64,128]{1,0:T(8,128)(2,1)S(1)} %get-tuple-element.224), kind=kOutput, calls=%fused_computation.110 | convolution fusion | flops 503373824 | bytes 3391496 | tf_op jit(solution)/shard_map/dot_general | solution.py:202
  207.1 13.4 %all-reduce.1 = (f32[1024]{0:T(1024)S(1)}, f32[1024]{0:T(1024)S(1)}, f32[]{:T(128)}) all-reduce(f32[1024]{0:T(1024)} %get-tuple-element.163, f32[1024]{0:T(1024)} %get-tuple-element.162, f32[]{:T(128)} %get-tuple-element.230), channel_id=1, replica_groups=mesh['tm'=8,'batch'=4] {'tm'}, use_global_device_ids=true, to_apply=%region_4.0 | all-reduce | flops 2049 | bytes 16392 | tf_op jit(solution)/shard_map/psum | solution.py:176
  220.5 1.5 fusion.60
  222.2 14.2 %while.22 = (s32[]{:T(128)}, bf16[2,512,1,128]{3,1,2,0:T(8,128)(2,1)S(1)}, s32[1024]{0:T(1024)}, s32[2]{0:T(128)}, bf16[1024,1,128]{0,2,1:T(8,128)(2,1)}, /*inde...) while((s32[]{:T(128)}, ...), condition=%wide.region_10.0_spmd.clone, body=%wide.region_7.10_spmd.clone.sunk | while | flops 273218560 | bytes 8147139 | solution.py:94
  222.2 1.2 dynamic_slice.56
  226.1 1.7 fusion.163
  229.4 1.2 dynamic_slice.56
  233.2 1.7 fusion.163
  236.5 1.1 fusion.119
  238.2 33.1 %reduce-scatter.3.cloned.1.call-done = f32[64,128]{1,0:T(8,128)} async-done(((f32[64,1024]{1,0:T(8,128)}), f32[64,128]{1,0:T(8,128)}) %reduce-scatter.3.cloned.1.call-update) | async-done | bytes 32784 | tf_op jit(solution)/shard_map/reduce_scatter | solution.py:200
  271.4 3.4 fusion.46
  274.8 1.4 fusion.16
  276.8 132.0 %all-reduce.6.cloned.1.call-done = f32[64,5120]{1,0:T(8,128)} async-done(((f32[64,5120]{1,0:T(8,128)}), f32[64,5120]{1,0:T(8,128)}) %all-reduce.6.cloned.1.call-update) | async-done | bytes 1310736 | tf_op jit(solution)/shard_map/psum | solution.py:218
  408.8 2.5 copy.87
  (152 shorter events, 27.5 us)
Async XLA Ops:
  7.2 1.3 copy-start
  7.2 137.6 %all-reduce.8.cloned.1.call-start = ((), (), s32[]{:S(2)}) async-start(), calls=%async_computation.5 | async-start | bytes 180224 | tf_op jit(solution)/shard_map/psum | solution.py:176
  8.5 30.9 %copy-start.5 = (bf16[5120,128]{1,0:T(8,128)(2,1)S(1)}, bf16[5120,128]{1,0:T(8,128)(2,1)}, u32[]{:S(2)}) copy-start(bf16[5120,128]{1,0:T(8,128)(2,1)} %param.32) | copy-start | bytes 3932164
  10.9 58.4 %collective-permute-start = (bf16[64,128]{1,0:T(8,128)(2,1)S(1)}, bf16[64,128]{1,0:T(8,128)(2,1)S(1)}, u32[]{:S(2)}, u32[]{:S(2)}) collective-permute-start(bf16[64,128]{1,0:T(8,128)(2,1)S(1)} %get-tuple-element.224), channel_id=1, source_target_pairs={{0,4},{4,8},{8,12},{12,16},{16,20},{20,24},{24,28},{1,5},{5,9},{9,... | collective-permute-start | bytes 49160 | tf_op jit(solution)/shard_map/ppermute | solution.py:21
  16.5 24.2 %copy-start.31 = (bf16[256]{0:T(256)(128)(2,1)}, bf16[256]{0:T(256)(128)(2,1)S(1)}, u32[]{:S(2)}) copy-start(bf16[256]{0:T(256)(128)(2,1)S(1)} %pad_maximum_fusion.9) | copy-start | bytes 1540
  39.4 1.3 copy-start.7
  40.7 1.3 copy-start.3
  40.7 1.7 copy-start.6
  44.0 1.5 copy-start.8
  48.3 3.6 copy-start.34
  48.3 4.2 %copy-start.15 = (bf16[64,5120]{1,0:T(8,128)(2,1)S(1)}, bf16[64,5120]{1,0:T(8,128)(2,1)}, u32[]{:S(2)}) copy-start(bf16[64,5120]{1,0:T(8,128)(2,1)} %param.35) | copy-start | bytes 1966084
  68.6 18.4 %copy-start.17 = (bf16[64,1024]{1,0:T(8,128)(2,1)}, bf16[64,1024]{1,0:T(8,128)(2,1)S(1)}, u32[]{:S(2)}) copy-start(bf16[64,1024]{1,0:T(8,128)(2,1)S(1)} %all_gather.16) | copy-start | bytes 393220
  68.6 18.4 %copy-start.25 = (bf16[64,896]{1,0:T(8,128)(2,1)}, bf16[64,896]{1,0:T(8,128)(2,1)S(1)}, u32[]{:S(2)}) copy-start(bf16[64,896]{1,0:T(8,128)(2,1)S(1)} %slice.122) | copy-start | bytes 344068
  69.3 0.6 copy-start.26
  69.9 18.1 %copy-start.2 = (f32[128,5120]{1,0:T(8,128)}, f32[128,5120]{1,0:T(8,128)S(1)}, u32[]{:S(2)}) copy-start(f32[128,5120]{1,0:T(8,128)S(1)} %get-tuple-element.227) | copy-start | bytes 7864324
  69.9 17.0 %copy-start.20 = (f32[3,130,128]{2,1,0:T(8,128)S(1)}, f32[3,130,128]{2,1,0:T(8,128)}, u32[]{:S(2)}) copy-start(f32[3,130,128]{2,1,0:T(8,128)} %pad_maximum_fusion.1) | copy-start | bytes 599044
  87.0 2.2 copy-start.4
  87.0 2.2 copy-start.27
  88.0 1.2 copy-start.12
  89.9 1.5 copy-start.1
  92.3 110.1 %reduce-scatter.5.cloned.1.call-start = ((), (), s32[]{:S(2)}) async-start(), calls=%async_computation.3 | async-start | bytes 294912 | tf_op jit(solution)/shard_map/reduce_scatter | solution.py:199
  102.3 42.5 %copy-start.28 = (f32[8,1,128]{2,1,0:T(1,128)}, f32[8,1,128]{2,1,0:T(1,128)S(1)}, u32[]{:S(2)}) copy-start(f32[8,1,128]{2,1,0:T(1,128)S(1)} %all-gather) | copy-start | bytes 12292
  144.8 5.7 %copy-start.10 = (bf16[5120,128]{1,0:T(8,128)(2,1)S(1)}, bf16[5120,128]{1,0:T(8,128)(2,1)}, u32[]{:S(2)}) copy-start(bf16[5120,128]{1,0:T(8,128)(2,1)} %param.39) | copy-start | bytes 3932164
  144.8 5.7 %copy-start.14 = (f32[3,5120]{1,0:T(4,128)S(1)}, f32[3,5120]{1,0:T(4,128)}, u32[]{:S(2)}) copy-start(f32[3,5120]{1,0:T(4,128)} %get-tuple-element.199) | copy-start | bytes 184324
  150.5 1.3 copy-start.9
  153.3 1.5 copy-start.11
  156.1 2.4 copy-start.30
  156.1 2.4 copy-start.29
  156.1 2.4 copy-start.13
  156.1 2.4 copy-start.32
  156.1 2.4 copy-start.33
  157.7 1.2 copy-start.18
  157.7 1.2 copy-start.21
  157.7 1.2 copy-start.35
  158.9 9.1 %copy-start.23 = (f32[128,64]{0,1:T(8,128)S(1)}, f32[128,64]{0,1:T(8,128)}, u32[]{:S(2)}) copy-start(f32[128,64]{0,1:T(8,128)} %fusion.20) | copy-start | bytes 98308
  169.1 102.3 %reduce-scatter.3.cloned.1.call-start = ((), (), s32[]{:S(2)}) async-start(), calls=%async_computation.2 | async-start | bytes 294912 | tf_op jit(solution)/shard_map/reduce_scatter | solution.py:200
  222.2 14.2 %copy-start.24 = (f32[128,64]{0,1:T(8,128)S(1)}, f32[128,64]{0,1:T(8,128)}, u32[]{:S(2)}) copy-start(f32[128,64]{0,1:T(8,128)} %fusion.26) | copy-start | bytes 98308
  222.2 49.2 %copy-start.16 = (bf16[64,5120]{1,0:T(8,128)(2,1)S(1)}, bf16[64,5120]{1,0:T(8,128)(2,1)}, u32[]{:S(2)}) copy-start(bf16[64,5120]{1,0:T(8,128)(2,1)} %param.43) | copy-start | bytes 1966084
  222.2 49.1 %copy-start.22 = (f32[64,128]{1,0:T(8,128)S(1)}, f32[64,128]{1,0:T(8,128)}, u32[]{:S(2)}) copy-start(f32[64,128]{1,0:T(8,128)} %get-tuple-element.231) | copy-start | bytes 98308
  227.8 1.0 copy-start.19
  234.9 1.0 copy-start.19
  237.6 171.2 %all-reduce.6.cloned.1.call-start = ((), (), s32[]{:S(2)}) async-start(), calls=%async_computation.4 | async-start | bytes 2621440 | tf_op jit(solution)/shard_map/psum | solution.py:218
Sparse Core Ops, SparseCore 0:
  92.4 52.2 all-reduce.7
  169.2 33.1 reduce-scatter.4
  237.7 33.6 reduce-scatter.2
  277.2 131.5 all-reduce.5
where the time goes:
time: 421 us; the launch traced here: 418 us
  waiting for transfers between devices  222 us (53%)
  blocking collectives  80.2 us (19%)
  matrix products  55.5 us (13%)
  local copies, waits for them, and re-layouts  17.6 us (4%)
  between operations  15.8 us (4%)
  other arithmetic  13.9 us (3%)
  loops' own time  7.68 us (2%)
  starting transfers between devices  4.87 us (1%)
    psum x1, waiting for transfers between devices, per_device(): lax.psum(partial_grad / normalizer / grad_root, ('tm', 'batch'))  132 us
    psum x1, waiting for transfers between devices, per_device(): lax.psum((jnp.sum(qkv_real[0] * qkv_real[0], axis=1), jnp.sum(qkv_real[1]...  33.2 us
    reduce_scatter x1, waiting for transfers between devices, per_device(): lax.psum_scatter(term_fake, 'tm', scatter_dimension=1, tiled=True)  33.1 us
    reduce_scatter x1, waiting for transfers between devices, per_device(): lax.psum_scatter(term_real, 'tm', scatter_dimension=1, tiled=True)  23.9 us
    psum x1, blocking collectives, per_device(): modul_real, modul_fake = lax.psum((share_real, share_fake), 'tm')  21.3 us
    psum x1, blocking collectives, per_device(): lax.psum((jnp.sum(qkv_real[0] * qkv_real[0], axis=1), jnp.sum(qkv_real[1]...  13.4 us
    all_gather x1, blocking collectives, per_device(): lax.all_gather(noisy_patch.astype(jnp.float32), 'tm', axis=1, tiled=True)  12.4 us
    dot_general x6, matrix products, fold_one(): main_part = jnp.dot(widened, wide_weight, precision=highest)  9.04 us
  transfers between devices with their start and end apart: 5, of which 4 were waited for; matrix products, arithmetic and copies ran while one was open for 8% of the time, Pallas kernels for 0%

commit v1 on v0

v1 whole, which is shorter than its diff:
```python
import functools
import math

import jax
import jax.numpy as jnp
from jax import lax
from jax.experimental import pallas as pl
from jax.experimental.pallas import tpu as pltpu
from jax.sharding import PartitionSpec as P

HD = 128
FREQ = 256
FTOK = 128


norm_floor = 0.05
gap_floor = 0.25
highest = lax.Precision.HIGHEST


MESH = pl.DeviceIdType.MESH
f32 = jnp.float32
bf16 = jnp.bfloat16


def greet(sizes):
    barrier = pltpu.get_barrier_semaphore()
    count = 0
    for axis, size in sizes.items():
        me = lax.axis_index(axis)
        for k in range(1, size):
            pl.semaphore_signal(
                barrier, inc=1, device_id={axis: lax.rem(me + k, size)}, device_id_type=MESH
            )
            count += 1
    pl.semaphore_wait(barrier, count)


def exchange(axis, size, source, slots, send, recv):
    me = lax.axis_index(axis)
    copies = []
    for k in range(1, size):
        peer = lax.rem(me + k, size)
        copy = pltpu.make_async_remote_copy(
            src_ref=source(peer),
            dst_ref=slots.at[me],
            send_sem=send.at[k],
            recv_sem=recv.at[k],
            device_id={axis: peer},
            device_id_type=MESH,
        )
        copy.start()
        copies.append(copy)
    return copies


def landed(copies):
    for copy in copies:
        copy.wait_recv()


def gone(copies):
    for copy in copies:
        copy.wait_send()


def sems(*sizes):
    return [pltpu.SemaphoreType.DMA((size,)) for size in sizes for _ in range(2)]


def comm_call(body, out_shape, scratch, collective_id, *args):
    vmem = pl.BlockSpec(memory_space=pltpu.VMEM)
    return pl.pallas_call(
        body,
        out_shape=out_shape,
        in_specs=[vmem] * len(args),
        out_specs=jax.tree.map(lambda _: vmem, out_shape),
        scratch_shapes=scratch,
        compiler_params=pltpu.CompilerParams(
            collective_id=collective_id, has_side_effects=True
        ),
    )(*args)


def start_kernel(n, noisy_ref, share_ref, patches_ref, modul_ref, parts, s1, r1, s2, r2, s3, r3):
    me = lax.axis_index("tm")
    greet({"tm": n})
    scatter = exchange("tm", n, lambda peer: share_ref.at[peer], parts, s1, r1)
    spread = exchange("tm", n, lambda peer: noisy_ref, patches_ref, s2, r2)
    patches_ref[me] = noisy_ref[...]
    parts[me] = share_ref[me]
    landed(scatter)
    modul_ref[me] = jnp.sum(parts[...], axis=0)
    collect = exchange("tm", n, lambda peer: modul_ref.at[me], modul_ref, s3, r3)
    landed(spread)
    landed(collect)
    gone(scatter)
    gone(spread)
    gone(collect)


def sums_kernel(n, own_ref, total_ref, parts, s1, r1):
    greet({"tm": n})
    spread = exchange("tm", n, lambda peer: own_ref, parts, s1, r1)
    parts[lax.axis_index("tm")] = own_ref[...]
    landed(spread)
    total_ref[...] = jnp.sum(parts[...], axis=0)
    gone(spread)


def terms_kernel(n, own_ref, total_ref, parts, s1, r1):
    me = lax.axis_index("tm")
    greet({"tm": n})
    scatter = exchange("tm", n, lambda peer: own_ref.at[peer], parts, s1, r1)
    parts[me] = own_ref[me]
    landed(scatter)
    total_ref[...] = jnp.sum(parts[...].astype(f32), axis=0)
    gone(scatter)


def grad_kernel(
    n, nb, count_all, grad_root, own_ref, gap_ref, grad_ref, norm_ref,
    parts, gaps, mixed, quarters, merged, s1, r1, s2, r2, s3, r3, s4, r4, s5, r5,
):
    me = lax.axis_index("tm")
    mine = lax.axis_index("batch")
    greet({"tm": n, "batch": nb})
    gap_copies = exchange("tm", n, lambda peer: gap_ref, gaps, s1, r1)
    scatter = exchange("tm", n, lambda peer: own_ref.at[peer], parts, s2, r2)
    gaps[me] = gap_ref[...]
    parts[me] = own_ref[me]
    landed(gap_copies)
    normalizer = jnp.maximum(jnp.sum(gaps[...], axis=0) / count_all, gap_floor)
    norm_ref[...] = normalizer
    landed(scatter)
    summed = jnp.sum(parts[...].astype(f32), axis=0) / normalizer[:1, :1] / grad_root
    mixed[...] = summed.reshape(mixed.shape).astype(bf16)
    across = exchange("batch", nb, lambda peer: mixed.at[peer], quarters, s3, r3)
    quarters[mine] = mixed[mine]
    landed(across)
    merged[mine] = jnp.sum(quarters[...].astype(f32), axis=0).astype(bf16)
    back = exchange("batch", nb, lambda peer: merged.at[mine], merged, s4, r4)
    landed(back)
    grad_ref[me] = merged[...]
    last = exchange("tm", n, lambda peer: merged, grad_ref, s5, r5)
    landed(last)
    for copies in (gap_copies, scatter, across, back, last):
        gone(copies)


def centered_table(embed_table):
    wide = embed_table.astype(f32)
    return wide - jnp.mean(wide, axis=1, keepdims=True)


def fold_heads(centered, modulation, weights):
    rows = jnp.concatenate([centered * (1.0 + modulation[1])[None, :], modulation[:1]], axis=0)
    high = rows.astype(bf16)
    low = (rows - high.astype(f32)).astype(bf16)
    both = jnp.concatenate([high, low], axis=0)
    folded = [jnp.dot(both, weight, preferred_element_type=f32) for weight in weights]
    folded = jnp.concatenate(folded, axis=1)
    return folded[: rows.shape[0]] + folded[rows.shape[0] :]


def project(stacked, gram, folded, width):
    kin_rows = stacked.shape[0]
    wide = stacked.astype(f32)
    variance = jnp.sum(wide * jnp.dot(gram, wide, precision=highest), axis=0)
    rscale = lax.rsqrt(jnp.maximum(variance, 0.0) + norm_floor)
    main = folded[:kin_rows]
    high = main.astype(bf16)
    low = (main - high.astype(f32)).astype(bf16)
    both = jnp.concatenate([high, low], axis=0)
    twice = jnp.concatenate([stacked, stacked], axis=0)
    base = lax.dot_general(
        twice, both, (((0,), (0,)), ((), ())), preferred_element_type=f32
    )
    full = rscale[:, None] * base + folded[kin_rows][None, :]
    return [full[:, i * width : (i + 1) * width] for i in range(3)]


def sinusoid(time_step):
    half_freq = FREQ // 2
    frequency = jnp.exp(-math.log(10000.0) * jnp.arange(half_freq, dtype=jnp.float32) / half_freq)
    angles = time_step.astype(jnp.float32) * frequency
    return jnp.concatenate([jnp.cos(angles), jnp.sin(angles)]).astype(jnp.bfloat16)


def rms_round(vector, total_sq, columns, gain_row):
    return (
        vector * lax.rsqrt(total_sq / columns + norm_floor)[:, None] * gain_row[None, :]
    ).astype(jnp.bfloat16)


def attend(query_norm, key_norm, value_norm):
    token_count = query_norm.shape[0]
    block_rows = min(512, token_count)
    frames = jnp.arange(token_count, dtype=jnp.int32) // FTOK

    def one_block(row_start):
        query_block = lax.dynamic_slice_in_dim(query_norm, row_start, block_rows, 0)
        scores = jnp.einsum(
            "qhd,khd->hqk", query_block, key_norm, preferred_element_type=jnp.float32
        ) / math.sqrt(HD)
        query_frames = lax.dynamic_slice_in_dim(frames, row_start, block_rows, 0)
        allowed = frames[None, :] <= query_frames[:, None]
        scores = jnp.where(allowed[None], scores, -1e30)
        row_peak = jnp.max(scores, axis=2, keepdims=True)
        exp_scores = jnp.exp(scores - row_peak)
        attn_probs = (exp_scores / jnp.sum(exp_scores, axis=2, keepdims=True)).astype(jnp.bfloat16)
        return jnp.einsum(
            "hqk,khd->qhd", attn_probs, value_norm, preferred_element_type=jnp.float32
        ).astype(jnp.bfloat16)

    starts = jnp.arange(token_count // block_rows, dtype=jnp.int32) * block_rows
    pieces = lax.map(one_block, starts)
    return pieces.reshape(token_count, query_norm.shape[1], query_norm.shape[2])


def per_device(
    hidden_states,
    gen_weight,
    noise_field,
    timesteps,
    embed_real,
    time_real,
    query_real,
    key_real,
    value_real,
    out_real,
    gain_real,
    proj_real,
    embed_fake,
    time_fake,
    query_fake,
    key_fake,
    value_fake,
    out_fake,
    gain_fake,
    proj_fake,
):
    devices = lax.axis_size("tm")
    frame_tokens = hidden_states.shape[1]
    tokens = frame_tokens * devices
    patch_rows = gen_weight.shape[0]
    time_step = timesteps[0]
    level_raw = time_step.astype(jnp.float32) / 1000.0
    noise_level = 5.0 * level_raw / (1.0 + 4.0 * level_raw)
    generated = lax.dot_general(
        gen_weight, hidden_states[0], (((1,), (1,)), ((), ())), preferred_element_type=f32
    ).astype(bf16)
    noisy_patch = (
        (1.0 - noise_level) * generated.astype(f32) + noise_level * noise_field[0].astype(f32)
    ).astype(bf16)
    sinus_wave = sinusoid(time_step)
    freq_rows = time_real.shape[0]
    own_wave = lax.dynamic_slice_in_dim(sinus_wave, lax.axis_index("tm") * freq_rows, freq_rows, 0)
    model_width = hidden_states.shape[2]
    part_width = model_width // devices
    shares = jnp.concatenate(
        [
            jnp.dot(own_wave[None], t.reshape(freq_rows, -1), preferred_element_type=f32).reshape(
                3, devices, part_width
            )
            for t in (time_real, time_fake)
        ]
    ).transpose(1, 0, 2)
    patches, modul = comm_call(
        functools.partial(start_kernel, devices),
        [
            jax.ShapeDtypeStruct((devices, patch_rows, frame_tokens), bf16),
            jax.ShapeDtypeStruct((devices, 6, part_width), f32),
        ],
        [pltpu.VMEM((devices, 6, part_width), f32), *sems(devices, devices, devices)],
        0,
        noisy_patch,
        shares,
    )
    modul = modul.transpose(1, 0, 2).reshape(6, model_width)
    all_patch = patches.transpose(1, 0, 2).reshape(patch_rows, tokens)
    prior_frame = jnp.pad(all_patch, ((0, 0), (frame_tokens, 0)))[:, :tokens]
    all_stacked = jnp.concatenate([all_patch, prior_frame], axis=0)
    local_width = query_real.shape[1]
    local_heads = local_width // HD
    columns = local_width * devices
    qkv = []
    embeds = []
    nets = (
        (embed_real, modul[:3], query_real, key_real, value_real, gain_real, out_real, proj_real),
        (embed_fake, modul[3:], query_fake, key_fake, value_fake, gain_fake, out_fake, proj_fake),
    )
    own_stacked = lax.dynamic_slice_in_dim(
        all_stacked, lax.axis_index("tm") * frame_tokens, frame_tokens, 1
    )
    direct = []
    for embed, modulation, query, key, value, _, _, proj in nets:
        centered = centered_table(embed)
        gram = jnp.dot(centered, centered.T, precision=lax.Precision.HIGH) / model_width
        folded = fold_heads(centered, modulation, (query, key, value))
        qkv.append(project(all_stacked, gram, folded, local_width))
        inner = lax.dot_general(
            proj, embed, (((1,), (1,)), ((), ())), preferred_element_type=f32
        )
        direct.append(jnp.dot(inner, own_stacked.astype(f32), precision=highest))
    squares = jnp.stack([jnp.sum(qkv[i][j] * qkv[i][j], axis=1) for i in (0, 1) for j in (0, 1)])
    norm_sums = comm_call(
        functools.partial(sums_kernel, devices),
        jax.ShapeDtypeStruct((4, tokens), f32),
        [pltpu.VMEM((devices, 4, tokens), f32), *sems(devices)],
        1,
        squares,
    )
    head_shape = (tokens, local_heads, HD)
    terms = []
    for i, (_, modulation, _, _, _, gain, out, proj) in enumerate(nets):
        attended = attend(
            rms_round(qkv[i][0], norm_sums[2 * i], columns, gain[0]).reshape(head_shape),
            rms_round(qkv[i][1], norm_sums[2 * i + 1], columns, gain[1]).reshape(head_shape),
            qkv[i][2].astype(bf16).reshape(head_shape),
        ).reshape(devices, frame_tokens, local_width)
        gated = proj.astype(f32) * modulation[2][None, :]
        high = gated.astype(bf16)
        low = (gated - high.astype(f32)).astype(bf16)
        folded_out = lax.dot_general(
            jnp.concatenate([high, low], axis=0), out, (((1,), (1,)), ((), ())),
            preferred_element_type=f32,
        )
        folded_out = folded_out[:patch_rows] + folded_out[patch_rows:]
        terms.append(
            jnp.einsum("rc,ntc->nrt", folded_out.astype(bf16), attended, preferred_element_type=f32)
        )
    own_terms = comm_call(
        functools.partial(terms_kernel, devices),
        jax.ShapeDtypeStruct((2 * patch_rows, frame_tokens), f32),
        [pltpu.VMEM((devices, 2 * patch_rows, frame_tokens), bf16), *sems(devices)],
        2,
        jnp.concatenate(terms, axis=1).astype(bf16),
    )
    velocity_real = own_terms[:patch_rows] + direct[0]
    velocity_fake = own_terms[patch_rows:] + direct[1]
    pred_real = noisy_patch.astype(f32) - noise_level * velocity_real
    pred_fake = noisy_patch.astype(f32) - noise_level * velocity_fake
    gap_local = jnp.sum(jnp.abs(generated.astype(f32) - pred_real))
    count_all = patch_rows * tokens
    batches = lax.axis_size("batch")
    grad_root = math.sqrt(batches * hidden_states.shape[0] * tokens)
    gap_diff = pred_fake - pred_real
    difference = gap_diff.astype(bf16)
    partial_grad = jnp.dot(difference, hidden_states[0], preferred_element_type=f32)
    partial_grad = partial_grad.astype(bf16).reshape(patch_rows, devices, part_width)
    quarter = patch_rows // batches
    piece = (batches, quarter, part_width)
    grad, norm = comm_call(
        functools.partial(grad_kernel, devices, batches, count_all, grad_root),
        [
            jax.ShapeDtypeStruct((devices, *piece), bf16),
            jax.ShapeDtypeStruct((8, 128), f32),
        ],
        [
            pltpu.VMEM((devices, patch_rows, part_width), bf16),
            pltpu.VMEM((devices, 8, 128), f32),
            pltpu.VMEM(piece, bf16),
            pltpu.VMEM(piece, bf16),
            pltpu.VMEM(piece, bf16),
            *sems(devices, devices, batches, batches, devices),
        ],
        3,
        partial_grad.transpose(1, 0, 2),
        jnp.broadcast_to(gap_local, (8, 128)),
    )
    weight_grad = grad.reshape(devices, patch_rows, part_width).transpose(1, 0, 2)
    weight_grad = weight_grad.reshape(patch_rows, model_width).astype(f32)
    dmd_gradient = (gap_diff / norm[0, 0])[None]
    return (dmd_gradient, weight_grad)


def solution(mesh):
    in_specs = (
        P("batch", "tm", None),
        P(),
        P("batch", None, "tm"),
        P("batch"),
        P(),
        P("tm", None, None),
        P(None, "tm"),
        P(None, "tm"),
        P(None, "tm"),
        P("tm", None),
        P(None, "tm"),
        P(),
        P(),
        P("tm", None, None),
        P(None, "tm"),
        P(None, "tm"),
        P(None, "tm"),
        P("tm", None),
        P(None, "tm"),
        P(),
    )
    out_specs = (P("batch", None, "tm"), P())
    return jax.shard_map(
        per_device, mesh=mesh, in_specs=in_specs, out_specs=out_specs, check_vma=False
    )
```

time: 421 us -> 147 us (0.35)
  waiting for transfers between devices: 222 us -> 0 us
  blocking collectives: 80.2 us -> 0 us
  Pallas kernels: 0 us -> 58.8 us
  matrix products: 55.5 us -> 31.9 us
  between operations: 15.8 us -> 2.04 us
  local copies, waits for them, and re-layouts: 17.6 us -> 28.2 us
  starting transfers between devices: 4.87 us -> 0 us
    psum x2 -> x0, waiting for transfers between devices: 165 us -> none  [the longest x1 132 us: per_device(): lax.psum(partial_grad / normalizer / grad_root, ('tm', 'batch'))]
    pallas_call x0 -> x4, Pallas kernels: none -> 58.8 us  [comm_call(): pl.pallas_call(body, out_shape=out_shape, in_specs=[vmem] * len(args), ou...]
    reduce_scatter x2 -> x0, waiting for transfers between devices: 57 us -> none  [the longest x1 33.1 us: per_device(): lax.psum_scatter(term_fake, 'tm', scatter_dimension=1, tiled=True)]
    all_gather x5 -> x0, blocking collectives: 45.5 us -> none  [the longest x1 12.4 us: per_device(): lax.all_gather(noisy_patch.astype(jnp.float32), 'tm', axis=1, tiled=True)]
    psum x2 -> x0, blocking collectives: 34.7 us -> none  [the longest x1 21.3 us: per_device(): modul_real, modul_fake = lax.psum((share_real, share_fake), 'tm')]
    dot_general x31 -> x23, matrix products: 45.8 us -> 18.6 us  [the longest x6 5.81 us: fold_heads(): jnp.dot(both, weight, preferred_element_type=f32)]
    unnamed x79 -> x60, local copies, waits for them, and re-layouts: 7.91 us -> 13.4 us
    reshape x0 -> x6, local copies, waits for them, and re-layouts: none -> 5.1 us  [the longest x2 2.85 us: per_device(): qkv[i][2].astype(bf16).reshape(head_shape)]
  transfers between devices with their start and end apart: 5 -> 0, of which waited for: 4 -> 0; matrix products, arithmetic and copies ran while one was open for 8% -> 0% of each run, Pallas kernels for 0% -> 0%
where the time goes in v1:
time: 147 us; the launch traced here: 146 us
  Pallas kernels  58.8 us (40%)
  matrix products  31.9 us (22%)
  local copies, waits for them, and re-layouts  28.2 us (19%)
  other arithmetic  17.5 us (12%)
  loops' own time  7.46 us (5%)
  between operations  2.04 us (1%)
    pallas_call x4, Pallas kernels, comm_call(): pl.pallas_call(body, out_shape=out_shape, in_specs=[vmem] * len(args), ou...  58.8 us
    unnamed x60, local copies, waits for them, and re-layouts  13.4 us
    another operation x2, loops' own time, attend(): pieces = lax.map(one_block, starts)  7.46 us
    dot_general x4, matrix products, one_block(): jnp.einsum('qhd,khd->hqk', query_block, key_norm, preferred_element_type=...  7.29 us
    dot_general x6, matrix products, fold_heads(): jnp.dot(both, weight, preferred_element_type=f32)  5.81 us
    dot_general x4, matrix products, one_block(): jnp.einsum('hqk,khd->qhd', attn_probs, value_norm, preferred_element_type...  4.82 us
    dot_general x2, matrix products, per_device(): jnp.dot(centered, centered.T, precision=lax.Precision.HIGH) / model_width  3.25 us
    dot_general x2, matrix products, per_device(): jnp.einsum('rc,ntc->nrt', folded_out.astype(bf16), attended, preferred_el...  2.98 us

profile of v1, /device:TPU:1, one launch (start us, length us, event | category | flops | bytes accessed | tf_op | source)
XLA Modules:
  0.0 145.8 jit_solution(12615215941096357297)
XLA Ops:
  1.5 1.3 copy.50
  5.3 1.2 fusion.79
  6.5 13.6 %shard_map.203 = (bf16[8,64,128]{2,1,0:T(8,128)(2,1)}, f32[8,6,640]{2,1,0:T(8,128)}) custom-call(bf16[64,128]{1,0:T(8,128)(2,1)} %get-tuple-element.218.noisy_ref, f32[8,6,640]{2,1,0:T(8,128)} %maximum_bitcast_fusion.share_ref), custom_call_target="tpu_custom_call" | custom-call | tf_op jit(solution)/shard_map/pallas_call | solution.py:73
  20.1 2.2 %fusion.108 = (f32[1,8,640]{2,0,1:T(1,128)}, f32[1,8,640]{2,0,1:T(1,128)}, f32[1,8,640]{2,0,1:T(1,128)S(1)}, f32[1,8,640]{2,0,1:T(1,128)S(1)}, f32[1,8,640]{2,0,1:T(1,128)S(1)}, /*index=5*/f32[1,8,640]{2,0,1:T(1,128)S(1)}) fusion(f32[6,8,640]{2,0,1:T(8,128)} %bitcast.225), kind=kLoop, calls=%fused_computation.192 | loop fusion | flops 10240 | bytes 245760 | tf_op jit(solution)/shard_map/slice | solution.py:322
  23.4 1.1 copy-done.21
  24.5 1.0 fusion.63
  25.8 1.0 fusion.62
  27.1 1.0 fusion.61
  29.0 1.5 %fusion.42 = f32[128,128]{1,0:T(8,128)S(1)} fusion(bf16[128,5120]{1,0:T(8,128)(2,1)S(1)} %copy-done.1, f32[128]{0:T(128)S(1)} %broadcast_multiply_fusion.1), kind=kOutput, calls=%fused_computation.72 | convolution fusion | flops 504643584 | bytes 1376768 | tf_op jit(solution)/shard_map/dot_general | solution.py:299
  31.4 1.1 copy-done.6
  33.8 1.1 copy-done.24
  34.9 1.0 fusion.60
  36.2 1.0 fusion.59
  37.5 0.9 fusion.58
  38.6 1.7 %fusion.41 = f32[128,128]{1,0:T(8,128)S(1)} fusion(bf16[128,5120]{1,0:T(8,128)(2,1)S(1)} %copy-done.2, f32[128]{0:T(128)S(1)} %broadcast_multiply_fusion), kind=kOutput, calls=%fused_computation.71 | convolution fusion | flops 504643584 | bytes 1376768 | tf_op jit(solution)/shard_map/dot_general | solution.py:299
  41.2 1.1 copy-done.4
  43.0 6.4 %shard_map.204 = f32[4,1024]{1,0:T(4,128)} custom-call(f32[4,1024]{1,0:T(4,128)} %pad_maximum_fusion.19.own_ref), custom_call_target="tpu_custom_call" | custom-call | tf_op jit(solution)/shard_map/pallas_call | solution.py:73
  49.5 0.9 add_rsqrt_fusion.2
  50.4 2.0 %fusion.65 = (bf16[1024,1,128]{0,2,1:T(8,128)(2,1)S(1)}, bf16[1024,1,128]{0,2,1:T(8,128)(2,1)}) fusion(f32[1024,384]{0,1:T(8,128)} %copy-done.6, f32[128]{0:T(128)S(1)} %get-tuple-element.214, f32[1024]{0:T(1024)S(1)} %bitcast.234, f32[128]{0:T(128)S(1)} %get-tuple-element.215, f32[1024]{0:T(1024)S(1)} %bitcast.235), kind=kLoop, calls=%fused_computation.110 | loop fusion | flops 786432 | bytes 1582080 | tf_op jit(solution)/shard_map/reshape | solution.py:319
  53.2 1.1 fusion.68
  54.3 0.8 copy.34
  55.9 13.0 %while.22 = (s32[]{:T(128)}, bf16[2,512,1,128]{3,1,2,0:T(8,128)(2,1)}, s32[1024]{0:T(1024)S(1)}, s32[2]{0:T(128)S(1)}, bf16[1024,1,128]{0,2,1:T(8,128)(2,1)}, /*...) while((s32[]{:T(128)}, ...), condition=%wide.region_11.12_spmd.clone, body=%wide.region_8.11_spmd.clone.sunk | while | flops 273218560 | bytes 8147639 | solution.py:217
  58.4 1.8 %fusion.140 = (f32[512]{0:T(512)S(1)}, f32[512,1024]{1,0:T(8,128)S(1)}) fusion(bf16[1024,1,128]{2,0,1:T(8,128)(2,1)} %get-tuple-element.373, bf16[1024,1,128]{0,2,1:T(8,128)(2,1)} %get-tuple-element.372, s32[]{:T(128)S(6)} %select_n.47, s32[512]{0:T(512)S(1)} %dynamic_slice.77, s32[1024]{0:T(1024)S(1)} %get-tuple-element.370), kind=kOutput, calls=%fused_computation.190.clone.1 | convolution fusion | flops 136314368 | bytes 2498564 | tf_op jit(solution)/shard_map/while/body/eval_jaxpr/qhd,khd->hqk/dot_general | solution.py:203
  61.2 1.2 fusion.142
  64.9 1.8 %fusion.140 = (f32[512]{0:T(512)S(1)}, f32[512,1024]{1,0:T(8,128)S(1)}) fusion(bf16[1024,1,128]{2,0,1:T(8,128)(2,1)} %get-tuple-element.373, bf16[1024,1,128]{0,2,1:T(8,128)(2,1)} %get-tuple-element.372, s32[]{:T(128)S(6)} %select_n.47, s32[512]{0:T(512)S(1)} %dynamic_slice.77, s32[1024]{0:T(1024)S(1)} %get-tuple-element.370), kind=kOutput, calls=%fused_computation.190.clone.1 | convolution fusion | flops 136314368 | bytes 2498564 | tf_op jit(solution)/shard_map/while/body/eval_jaxpr/qhd,khd->hqk/dot_general | solution.py:203
  67.7 1.2 fusion.142
  68.9 1.0 fusion.34
  70.7 1.8 %fusion.39 = bf16[8,64,128]{2,1,0:T(8,128)(2,1)} fusion(bf16[8,128,128]{2,1,0:T(8,128)(2,1)} %bitcast.29, f32[128,128]{1,0:T(8,128)S(1)} %fusion.22), kind=kOutput, calls=%fused_computation.69 | convolution fusion | flops 16859136 | bytes 458752 | tf_op jit(solution)/shard_map/rc,ntc->nrt/dot_general | solution.py:331
  72.6 0.9 fusion.67
  73.5 1.8 %copy.36 = bf16[1024,1,128]{2,0,1:T(8,128)(2,1)} copy(bf16[1024,1,128]{0,2,1:T(8,128)(2,1)} %get-tuple-element.198) | data formatting | bytes 524288
  75.3 1.8 %fusion.69 = bf16[1024,1,128]{0,2,1:T(8,128)(2,1)} fusion(f32[1024,384]{0,1:T(8,128)} %copy-done.4), kind=kLoop, calls=%fused_computation.114 | loop fusion | bytes 524288 | tf_op jit(solution)/shard_map/reshape | solution.py:320
  77.1 1.8 %copy.37 = bf16[1024,1,128]{2,0,1:T(8,128)(2,1)} copy(bf16[1024,1,128]{0,2,1:T(8,128)(2,1)} %fusion.69) | data formatting | bytes 524288
  79.6 13.1 %while.23 = (s32[]{:T(128)}, bf16[2,512,1,128]{3,1,2,0:T(8,128)(2,1)}, s32[1024]{0:T(1024)S(1)}, s32[2]{0:T(128)S(1)}, bf16[1024,1,128]{0,2,1:T(8,128)(2,1)}, /*...) while((s32[]{:T(128)}, ...), condition=%wide.region_15.16_spmd.clone, body=%wide.region_12.15_spmd.clone.sunk | while | flops 273218560 | bytes 8147639 | solution.py:217
  82.2 1.8 %fusion.144 = (f32[512]{0:T(512)S(1)}, f32[512,1024]{1,0:T(8,128)S(1)}) fusion(bf16[1024,1,128]{2,0,1:T(8,128)(2,1)} %get-tuple-element.343, bf16[1024,1,128]{0,2,1:T(8,128)(2,1)} %get-tuple-element.342, s32[]{:T(128)S(6)} %select_n.48, s32[512]{0:T(512)S(1)} %dynamic_slice.80, s32[1024]{0:T(1024)S(1)} %get-tuple-element.340), kind=kOutput, calls=%fused_computation.191.clone.1 | convolution fusion | flops 136314368 | bytes 2498564 | tf_op jit(solution)/shard_map/while/body/eval_jaxpr/qhd,khd->hqk/dot_general | solution.py:203
  85.0 1.2 fusion.146
  88.7 1.8 %fusion.144 = (f32[512]{0:T(512)S(1)}, f32[512,1024]{1,0:T(8,128)S(1)}) fusion(bf16[1024,1,128]{2,0,1:T(8,128)(2,1)} %get-tuple-element.343, bf16[1024,1,128]{0,2,1:T(8,128)(2,1)} %get-tuple-element.342, s32[]{:T(128)S(6)} %select_n.48, s32[512]{0:T(512)S(1)} %dynamic_slice.80, s32[1024]{0:T(1024)S(1)} %get-tuple-element.340), kind=kOutput, calls=%fused_computation.191.clone.1 | convolution fusion | flops 136314368 | bytes 2498564 | tf_op jit(solution)/shard_map/while/body/eval_jaxpr/qhd,khd->hqk/dot_general | solution.py:203
  91.5 1.2 fusion.146
  92.7 1.4 fusion.33
  94.8 1.2 fusion.40
  96.7 8.0 %shard_map.205 = f32[128,128]{1,0:T(8,128)} custom-call(bf16[8,128,128]{2,1,0:T(8,128)(2,1)} %pad_maximum_fusion.14.own_ref), custom_call_target="tpu_custom_call" | custom-call | tf_op jit(solution)/shard_map/pallas_call | solution.py:73
  105.4 1.7 %abs_reduce_fusion = (f32[]{:T(128)}, f32[64,128]{1,0:T(8,128)S(1)}) fusion(f32[64,128]{1,0:T(8,128)S(1)} %copy-done.16, f32[64,128]{1,0:T(8,128)S(1)} %fusion.110, s32[]{:T(128)S(6)} %select_n.37, bf16[64,1024]{1,0:T(8,128)(2,1)S(1)} %copy_bitcast_fusion, bf16[64,1024]{1,0:T(8,128)(2,1)S(1)} %pad_slice_fusion, f32[128,128]{1,0:T(8,128)} %shard_map.205, ...), kind=kOutput, calls=%fused_computation.141 | convolution fusion | flops 12705791 | bytes 409612 | tf_op jit(solution)/shard_map/dot_general | solution.py:305
  108.2 0.9 copy.63
  109.1 1.2 broadcast_in_dim.17.gap_ref
  110.3 30.8 %shard_map.206 = (bf16[8,4,16,640]{3,2,1,0:T(8,128)(2,1)}, f32[8,128]{1,0:T(8,128)}) custom-call(bf16[8,64,640]{2,1,0:T(8,128)(2,1)} %bitcast.214, f32[8,128]{1,0:T(8,128)} %broadcast_in_dim.17.gap_ref), custom_call_target="tpu_custom_call" | custom-call | tf_op jit(solution)/shard_map/pallas_call | solution.py:73
  141.2 1.2 convert_bitcast_fusion
  142.3 1.1 copy.52
  143.5 1.2 slice.167
  144.7 1.2 divide_bitcast_fusion
  (123 shorter events, 22.2 us)
Async XLA Ops:
  0.6 4.6 %copy-start = (bf16[1,128,5120]{2,1,0:T(8,128)(2,1)S(1)}, bf16[1,128,5120]{2,1,0:T(8,128)(2,1)}, u32[]{:S(2)}) copy-start(bf16[1,128,5120]{2,1,0:T(8,128)(2,1)} %param.24) | copy-start | bytes 3932164
  2.7 1.2 copy-start.9
  4.0 1.3 copy-start.10
  4.0 1.3 copy-start.18
  4.5 17.8 %copy-start.1 = (bf16[128,5120]{1,0:T(8,128)(2,1)S(1)}, bf16[128,5120]{1,0:T(8,128)(2,1)}, u32[]{:S(2)}) copy-start(bf16[128,5120]{1,0:T(8,128)(2,1)} %param.28) | copy-start | bytes 3932164
  23.1 1.3 copy-start.21
  24.5 1.3 copy-start.22
  25.8 1.3 copy-start.23
  28.1 0.9 copy-start.17
  31.0 1.7 %copy-start.2 = (bf16[128,5120]{1,0:T(8,128)(2,1)S(1)}, bf16[128,5120]{1,0:T(8,128)(2,1)}, u32[]{:S(2)}) copy-start(bf16[128,5120]{1,0:T(8,128)(2,1)} %param.36) | copy-start | bytes 3932164
  31.4 1.1 copy-start.6
  33.6 1.3 copy-start.24
  34.9 1.3 copy-start.25
  36.2 1.3 copy-start.26
  40.7 9.7 %copy-start.19 = (f32[2,128]{1,0:T(2,128)S(1)}, f32[2,128]{1,0:T(2,128)}, u32[]{:S(2)}) copy-start(f32[2,128]{1,0:T(2,128)} %param.34) | copy-start | bytes 3076
  41.2 1.2 copy-start.4
  55.9 13.0 %copy-start.7 = (bf16[64,5120]{1,0:T(8,128)(2,1)S(1)}, bf16[64,5120]{1,0:T(8,128)(2,1)}, u32[]{:S(2)}) copy-start(bf16[64,5120]{1,0:T(8,128)(2,1)} %param.35) | copy-start | bytes 1966084
  60.2 1.0 copy-start.15
  66.7 1.0 copy-start.15
  68.9 1.3 copy-start.27
  70.2 2.3 %copy-start.20 = (f32[2,128]{1,0:T(2,128)S(1)}, f32[2,128]{1,0:T(2,128)}, u32[]{:S(2)}) copy-start(f32[2,128]{1,0:T(2,128)} %param.42) | copy-start | bytes 3076
  70.2 2.3 %copy-start.5 = (f32[1024,384]{0,1:T(8,128)S(1)}, f32[1024,384]{0,1:T(8,128)}, u32[]{:S(2)}) copy-start(f32[1024,384]{0,1:T(8,128)} %copy-done.4) | copy-start | bytes 4718596
  84.0 1.0 copy-start.14
  90.5 1.0 copy-start.14
  92.7 1.5 %copy-start.28 = (bf16[128,5120]{1,0:T(8,128)(2,1)S(1)}, bf16[128,5120]{1,0:T(8,128)(2,1)}, u32[]{:S(2)}) copy-start(bf16[128,5120]{1,0:T(8,128)(2,1)} %param.41) | copy-start | bytes 3932164
  94.2 1.7 %copy-start.11 = (bf16[8,64,128]{2,1,0:T(8,128)(2,1)S(1)}, bf16[8,64,128]{2,1,0:T(8,128)(2,1)}, u32[]{:S(2)}) copy-start(bf16[8,64,128]{2,1,0:T(8,128)(2,1)} %fusion.39) | copy-start | bytes 393220
  94.8 10.5 %copy-start.12 = (bf16[64,128]{1,0:T(8,128)(2,1)S(1)}, bf16[64,128]{1,0:T(8,128)(2,1)}, u32[]{:S(2)}) copy-start(bf16[64,128]{1,0:T(8,128)(2,1)} %get-tuple-element.218.noisy_ref) | copy-start | bytes 49156
  104.7 0.8 copy-start.16
  104.7 2.4 %copy-start.3 = (bf16[128,5120]{1,0:T(8,128)(2,1)S(1)}, bf16[128,5120]{1,0:T(8,128)(2,1)}, u32[]{:S(2)}) copy-start(bf16[128,5120]{1,0:T(8,128)(2,1)} %param.36) | copy-start | bytes 3932164
  104.7 2.4 %copy-start.8 = (bf16[64,5120]{1,0:T(8,128)(2,1)S(1)}, bf16[64,5120]{1,0:T(8,128)(2,1)}, u32[]{:S(2)}) copy-start(bf16[64,5120]{1,0:T(8,128)(2,1)} %param.43) | copy-start | bytes 1966084
  105.4 2.2 %copy-start.13 = (f32[128,128]{1,0:T(8,128)S(1)}, f32[128,128]{1,0:T(8,128)}, u32[]{:S(2)}) copy-start(f32[128,128]{1,0:T(8,128)} %shard_map.205) | copy-start | bytes 196612

commit v2 on v0

v2 whole, which is shorter than its diff:
```python
import functools
import math

import jax
import jax.numpy as jnp
from jax import lax
from jax.experimental import pallas as pl
from jax.experimental.pallas import tpu as pltpu
from jax.sharding import PartitionSpec as P

HD = 128
FREQ = 256
FTOK = 128


norm_floor = 0.05
gap_floor = 0.25
highest = lax.Precision.HIGHEST


MESH = pl.DeviceIdType.MESH
f32 = jnp.float32
bf16 = jnp.bfloat16


def greet(sizes):
    barrier = pltpu.get_barrier_semaphore()
    count = 0
    for axis, size in sizes.items():
        me = lax.axis_index(axis)
        for k in range(1, size):
            pl.semaphore_signal(
                barrier, inc=1, device_id={axis: lax.rem(me + k, size)}, device_id_type=MESH
            )
            count += 1
    pl.semaphore_wait(barrier, count)


def exchange(axis, size, source, slots, send, recv):
    me = lax.axis_index(axis)
    copies = []
    for k in range(1, size):
        peer = lax.rem(me + k, size)
        copy = pltpu.make_async_remote_copy(
            src_ref=source(peer),
            dst_ref=slots.at[me],
            send_sem=send.at[k],
            recv_sem=recv.at[k],
            device_id={axis: peer},
            device_id_type=MESH,
        )
        copy.start()
        copies.append(copy)
    return copies


def landed(copies):
    for copy in copies:
        copy.wait_recv()


def gone(copies):
    for copy in copies:
        copy.wait_send()


def sems(*sizes):
    return [pltpu.SemaphoreType.DMA((size,)) for size in sizes for _ in range(2)]


def split(wide):
    high = wide.astype(bf16)
    return high, (wide - high.astype(f32)).astype(bf16)


def dot_nt(left, right):
    return lax.dot_general(left, right, (((1,), (1,)), ((), ())), preferred_element_type=f32)


def dot(left, right):
    return jnp.dot(left, right, preferred_element_type=f32)


def main_kernel(n, nb, part, level_ref, noisy_ref, made_ref, share_ref, gain_ref, *refs):
    big, refs = refs[:13], refs[13:]
    (dmd_ref, weight_ref), refs = refs[:2], refs[2:]
    held, refs = refs[:13], refs[13:]
    (load_sem, patches, parts, modul, fold, gate_fold, gram, inner, stack, qkv, squares,
     square_parts, keys, terms, term_parts, gap, gaps, halves, partner, across_chips, reduced,
     chip_parts, mixed, quarters, merged, grad) = refs[:26]
    sem = refs[26:]
    me = lax.axis_index("tm")
    mine = lax.axis_index("batch")
    core, chip = lax.rem(me, 2), lax.div(me, 2)
    chips = n // 2
    patch_rows, frame = noisy_ref.shape
    tokens = n * frame
    width = held[0].shape[1]
    chunks = width // part
    loads = []
    for i, (source, target) in enumerate(zip(big, held)):
        load = pltpu.make_async_copy(source, target, load_sem.at[i])
        load.start()
        loads.append(load)
    nets = [held[6 * i : 6 * i + 6] for i in (0, 1)]
    hidden = held[12]

    greet({"tm": n, "batch": nb})
    scatter = exchange("tm", n, lambda peer: share_ref.at[peer], parts, sem[0], sem[1])
    spread = exchange("tm", n, lambda peer: noisy_ref, patches, sem[2], sem[3])
    parts[me] = share_ref[me]
    patches[me] = noisy_ref[...]
    landed(scatter)
    modul[me] = jnp.sum(parts[...], axis=0)
    collect = exchange("tm", n, lambda peer: modul.at[me], modul, sem[4], sem[5])

    def columns(s):
        return pl.ds(pl.multiple_of(s * part, 128), part)

    means = []
    for i, (embed, proj, query, key, value, out) in enumerate(nets):
        loads[6 * i].wait()
        loads[6 * i + 1].wait()
        mean = jnp.sum(embed[...].astype(f32), axis=1, keepdims=True) / width
        means.append(mean)
        gram[i] = jnp.zeros(gram.shape[1:], f32)
        inner[i] = jnp.zeros(inner.shape[1:], f32)

        def gram_step(s, carry):
            table = embed[:, columns(s)]
            high, low = split(table.astype(f32) - mean)
            own = dot_nt(high, high)
            cross = dot_nt(high, low)
            gram[i] += own + cross + cross.T
            inner[i] += dot_nt(proj[:, columns(s)], table)
            return carry

        lax.fori_loop(0, chunks, gram_step, 0)

    landed(spread)
    kin = 2 * patch_rows
    for s in range(n):
        at = slice(s * frame, (s + 1) * frame)
        now = patches[s]
        before = patches[s - 1] if s else jnp.zeros_like(now)
        both = jnp.concatenate([now, before], axis=0)
        stack[:kin, at] = both
        stack[kin:, at] = both
    landed(collect)

    head = qkv.shape[1] // 3
    for i, (embed, proj, query, key, value, out) in enumerate(nets):
        for j in range(2, 6):
            loads[6 * i + j].wait()
        mean = means[i]
        fold[...] = jnp.zeros_like(fold)
        gate_fold[i] = jnp.zeros(gate_fold.shape[1:], f32)

        def fold_step(s, carry):
            at = columns(s)
            rows = modul[s]
            shift, scale, gate = (rows[3 * i + j : 3 * i + j + 1] for j in range(3))
            high, low = split((embed[:, at].astype(f32) - mean) * (1.0 + scale))
            shift_high, shift_low = split(jnp.broadcast_to(shift, (16, part)))
            left = jnp.concatenate([high, low, shift_high, shift_low], axis=0)
            right = jnp.concatenate([query[at, :], key[at, :], value[at, :]], axis=1)
            fold[...] += dot(left, right)
            high, low = split(proj[:, at].astype(f32) * gate)
            gate_fold[i] += dot_nt(jnp.concatenate([high, low], axis=0), out[:, at])
            return carry

        lax.fori_loop(0, chunks, fold_step, 0)
        folded = (fold[:kin] + fold[kin : 2 * kin]).T
        offset = (fold[2 * kin : 2 * kin + 8] + fold[2 * kin + 16 : 2 * kin + 24]).T[:, :1]
        gram_pair = jnp.concatenate(split(gram[i] / width), axis=1)
        fold_pair = jnp.concatenate(split(folded), axis=1)

        for s in range(n):
            at = slice(s * frame, (s + 1) * frame)
            pair = stack[:, at]
            variance = jnp.sum(pair[:kin].astype(f32) * dot(gram_pair, pair), axis=0, keepdims=True)
            rscale = lax.rsqrt(jnp.maximum(variance, 0.0) + norm_floor)
            full = dot(fold_pair, pair) * rscale + offset
            qkv[i, :, at] = full
            for j in range(2):
                rows = full[j * head : (j + 1) * head]
                squares[2 * i + j : 2 * i + j + 1, at] = jnp.sum(rows * rows, axis=0, keepdims=True)

    sums = exchange("tm", n, lambda peer: squares, square_parts, sem[6], sem[7])
    square_parts[me] = squares[...]
    landed(sums)
    inverse = lax.rsqrt(jnp.sum(square_parts[...], axis=0) / (head * n) + norm_floor)

    block = 2 * frame
    groups = min(4, tokens // block)
    per_group = tokens // block // groups
    for i in range(2):
        for s in range(n):
            at = slice(s * frame, (s + 1) * frame)
            gained = qkv[i, head : 2 * head, at] * inverse[2 * i + 1 : 2 * i + 2, at]
            keys[i, at, :] = (gained * gain_ref[i, :, 1:2]).T.astype(bf16)
            gained = qkv[i, :head, at] * inverse[2 * i : 2 * i + 1, at]
            qkv[i, :head, at] = gained * gain_ref[i, :, 0:1]
    fold_outs = [
        (gate_fold[i, :patch_rows] + gate_fold[i, patch_rows:]).astype(bf16) for i in range(2)
    ]
    for group in range(groups):
        length = (group + 1) * per_group * block

        def block_step(b, carry):
            at = pl.ds(pl.multiple_of(b * block, block), block)
            for i in range(2):
                query = qkv[i, :head, at].astype(bf16)
                scores = dot(keys[i, :length], query)
                low = (length - per_group * block)
                key_frame = (lax.broadcasted_iota(jnp.int32, (length - low, block), 0) + low) // frame
                query_frame = (
                    lax.broadcasted_iota(jnp.int32, (length - low, block), 1) + b * block
                ) // frame
                edge = jnp.where(key_frame <= query_frame, scores[low:], -1e30)
                if low:
                    scores = jnp.concatenate([scores[:low], edge], axis=0)
                else:
                    scores = edge
                peak = jnp.max(scores, axis=0, keepdims=True)
                powers = jnp.exp((scores - peak) * (1.0 / math.sqrt(HD)))
                total = jnp.sum(powers, axis=0, keepdims=True)
                values = qkv[i, 2 * head :, :length].astype(bf16)
                attended = dot(values, powers.astype(bf16)) / total
                term = dot(fold_outs[i], attended.astype(bf16)).astype(bf16)
                for j in range(2):
                    terms[2 * b + j, i * patch_rows : (i + 1) * patch_rows] = term[
                        :, j * frame : (j + 1) * frame
                    ]
            return carry

        if per_group == 1:
            block_step(group, 0)
        else:
            lax.fori_loop(group * per_group, (group + 1) * per_group, block_step, 0)

    give = exchange("tm", n, lambda peer: terms.at[peer], term_parts, sem[8], sem[9])
    term_parts[me] = terms[me]
    own = stack[:, pl.ds(pl.multiple_of(me * frame, frame), frame)]
    direct = [dot(jnp.concatenate(split(inner[i]), axis=1), own) for i in range(2)]
    noisy = noisy_ref[...].astype(f32)
    level = level_ref[:1, :1]
    landed(give)
    summed = jnp.sum(term_parts[...].astype(f32), axis=0)
    pred_real = noisy - level * (summed[:patch_rows] + direct[0])
    pred_fake = noisy - level * (summed[patch_rows:] + direct[1])
    difference = pred_fake - pred_real
    distance = jnp.abs(made_ref[...].astype(f32) - pred_real)
    distance = jnp.sum(jnp.sum(distance, axis=0, keepdims=True), axis=1, keepdims=True)
    gap[...] = jnp.broadcast_to(distance, gap.shape)
    gap_copies = exchange("tm", n, lambda peer: gap, gaps, sem[10], sem[11])
    gaps[me] = gap[...]
    loads[12].wait()
    rounded = difference.astype(bf16)
    for s in range(n):
        if s < chunks:
            piece = dot(rounded, hidden[:, s * part : (s + 1) * part]).astype(bf16)
        else:
            piece = jnp.zeros(halves.shape[2:], bf16)
        halves[s % 2, s // 2] = piece
    swap = pltpu.make_async_remote_copy(
        src_ref=halves.at[1 - core],
        dst_ref=partner,
        send_sem=sem[12].at[0],
        recv_sem=sem[12].at[1],
        device_id={"tm": me + 1 - 2 * core},
        device_id_type=MESH,
    )
    swap.start()
    swap.wait_recv()
    for k in range(chips):
        reduced[k] = (halves[core, k].astype(f32) + partner[k].astype(f32)).astype(bf16)

    def between_chips(source, slots, send, recv):
        copies = []
        for k in range(1, chips):
            peer = lax.rem(chip + k, chips)
            copy = pltpu.make_async_remote_copy(
                src_ref=source(peer),
                dst_ref=slots(chip),
                send_sem=send.at[k],
                recv_sem=recv.at[k],
                device_id={"tm": 2 * peer + core},
                device_id_type=MESH,
            )
            copy.start()
            copies.append(copy)
        return copies

    chip_copies = between_chips(
        lambda peer: reduced.at[peer], lambda at: chip_parts.at[at], sem[13], sem[14]
    )
    chip_parts[chip] = reduced[chip]
    landed(gap_copies)
    normalizer = jnp.maximum(jnp.sum(gaps[...], axis=0) / (patch_rows * tokens), gap_floor)[:1, :1]
    dmd_ref[...] = difference / normalizer
    landed(chip_copies)
    grad_root = math.sqrt(nb * tokens)
    total = jnp.sum(chip_parts[...].astype(f32), axis=0) / normalizer / grad_root
    mixed[...] = total.reshape(mixed.shape).astype(bf16)
    across = exchange("batch", nb, lambda peer: mixed.at[peer], quarters, sem[15], sem[16])
    quarters[mine] = mixed[mine]
    landed(across)
    merged[mine] = jnp.sum(quarters[...].astype(f32), axis=0).astype(bf16)
    back = exchange("batch", nb, lambda peer: merged.at[mine], merged, sem[17], sem[18])
    landed(back)
    grad[core, chip] = merged[...]
    last = between_chips(lambda peer: merged, lambda at: grad.at[core, at], sem[19], sem[20])
    landed(last)
    share = pltpu.make_async_remote_copy(
        src_ref=grad.at[core],
        dst_ref=grad.at[core],
        send_sem=sem[12].at[2],
        recv_sem=sem[12].at[3],
        device_id={"tm": me + 1 - 2 * core},
        device_id_type=MESH,
    )
    share.start()
    share.wait_recv()
    for s in range(chunks):
        piece = grad[s % 2, s // 2].astype(f32)
        weight_ref[:, s * part : (s + 1) * part] = piece.reshape(patch_rows, part)
    swap.wait_send()
    share.wait_send()
    for copies in (
        scatter, spread, collect, sums, give, gap_copies, chip_copies, across, back, last
    ):
        gone(copies)


def sinusoid(time_step):
    half_freq = FREQ // 2
    frequency = jnp.exp(-math.log(10000.0) * jnp.arange(half_freq, dtype=jnp.float32) / half_freq)
    angles = time_step.astype(jnp.float32) * frequency
    return jnp.concatenate([jnp.cos(angles), jnp.sin(angles)]).astype(jnp.bfloat16)


def per_device(
    hidden_states,
    gen_weight,
    noise_field,
    timesteps,
    embed_real,
    time_real,
    query_real,
    key_real,
    value_real,
    out_real,
    gain_real,
    proj_real,
    embed_fake,
    time_fake,
    query_fake,
    key_fake,
    value_fake,
    out_fake,
    gain_fake,
    proj_fake,
):
    devices = lax.axis_size("tm")
    frame_tokens = hidden_states.shape[1]
    tokens = frame_tokens * devices
    patch_rows = gen_weight.shape[0]
    time_step = timesteps[0]
    level_raw = time_step.astype(jnp.float32) / 1000.0
    noise_level = 5.0 * level_raw / (1.0 + 4.0 * level_raw)
    generated = lax.dot_general(
        gen_weight, hidden_states[0], (((1,), (1,)), ((), ())), preferred_element_type=f32
    ).astype(bf16)
    noisy_patch = (
        (1.0 - noise_level) * generated.astype(f32) + noise_level * noise_field[0].astype(f32)
    ).astype(bf16)
    sinus_wave = sinusoid(time_step)
    freq_rows = time_real.shape[0]
    own_wave = lax.dynamic_slice_in_dim(sinus_wave, lax.axis_index("tm") * freq_rows, freq_rows, 0)
    model_width = hidden_states.shape[2]
    batches = lax.axis_size("batch")
    part = -(-model_width // (devices * 128)) * 128
    while model_width % part:
        part += 128
    padding = ((0, 0), (0, devices * part - model_width))
    shares = jnp.concatenate(
        [
            jnp.dot(own_wave[None], t.reshape(freq_rows, -1), preferred_element_type=f32).reshape(
                3, model_width
            )
            for t in (time_real, time_fake)
        ]
    )
    shares = jnp.pad(shares, padding).reshape(6, devices, part).transpose(1, 0, 2)
    n, chips, quarter, head = devices, devices // 2, patch_rows // batches, query_real.shape[1]
    kin = 2 * patch_rows
    big = (
        embed_real, proj_real, query_real, key_real, value_real, out_real,
        embed_fake, proj_fake, query_fake, key_fake, value_fake, out_fake,
        hidden_states[0],
    )
    vm = pltpu.VMEM
    scratch = [
        *[vm(array.shape, array.dtype) for array in big],
        pltpu.SemaphoreType.DMA((len(big),)),
        vm((n, patch_rows, frame_tokens), bf16),
        vm((n, 6, part), f32),
        vm((n, 6, part), f32),
        vm((2 * kin + 32, 3 * head), f32),
        vm((2, kin, head), f32),
        vm((2, kin, kin), f32),
        vm((2, patch_rows, kin), f32),
        vm((2 * kin, tokens), bf16),
        vm((2, 3 * head, tokens), f32),
        vm((4, tokens), f32),
        vm((n, 4, tokens), f32),
        vm((2, tokens, head), bf16),
        vm((n, kin, frame_tokens), bf16),
        vm((n, kin, frame_tokens), bf16),
        vm((8, 128), f32),
        vm((n, 8, 128), f32),
        vm((2, chips, patch_rows, part), bf16),
        vm((chips, patch_rows, part), bf16),
        vm((8, 128), f32),
        vm((chips, patch_rows, part), bf16),
        vm((chips, patch_rows, part), bf16),
        vm((batches, quarter, part), bf16),
        vm((batches, quarter, part), bf16),
        vm((batches, quarter, part), bf16),
        vm((2, chips, batches, quarter, part), bf16),
        *sems(n, n, n, n, n, n),
        pltpu.SemaphoreType.DMA((4,)),
        *sems(chips, batches, batches, chips),
    ]
    vmem = pl.BlockSpec(memory_space=pltpu.VMEM)
    dmd, weight_grad = pl.pallas_call(
        functools.partial(main_kernel, devices, batches, part),
        out_shape=[
            jax.ShapeDtypeStruct((patch_rows, frame_tokens), f32),
            jax.ShapeDtypeStruct((patch_rows, model_width), f32),
        ],
        in_specs=[vmem] * 5 + [pl.BlockSpec(memory_space=pl.ANY)] * len(big),
        out_specs=[vmem, vmem],
        scratch_shapes=scratch,
        compiler_params=pltpu.CompilerParams(
            collective_id=0, has_side_effects=True, vmem_limit_bytes=60 * 1024 * 1024
        ),
    )(
        jnp.broadcast_to(noise_level, (8, 128)),
        noisy_patch,
        generated,
        shares,
        jnp.stack([gain_real.T, gain_fake.T]),
        *big,
    )
    return (dmd[None], weight_grad)


def solution(mesh):
    in_specs = (
        P("batch", "tm", None),
        P(),
        P("batch", None, "tm"),
        P("batch"),
        P(),
        P("tm", None, None),
        P(None, "tm"),
        P(None, "tm"),
        P(None, "tm"),
        P("tm", None),
        P(None, "tm"),
        P(),
        P(),
        P("tm", None, None),
        P(None, "tm"),
        P(None, "tm"),
        P(None, "tm"),
        P("tm", None),
        P(None, "tm"),
        P(),
    )
    out_specs = (P("batch", None, "tm"), P())
    return jax.shard_map(
        per_device, mesh=mesh, in_specs=in_specs, out_specs=out_specs, check_vma=False
    )
```

time: 421 us -> 74.2 us (0.18)
  waiting for transfers between devices: 222 us -> 0 us
  blocking collectives: 80.2 us -> 0 us
  Pallas kernels: 0 us -> 62.3 us
  matrix products: 55.5 us -> 3.37 us
  between operations: 15.8 us -> 1.46 us
  other arithmetic: 13.9 us -> 1.46 us
  local copies, waits for them, and re-layouts: 17.6 us -> 5.29 us
  loops' own time: 7.68 us -> 0 us
  starting transfers between devices: 4.87 us -> 0 us
    psum x2 -> x0, waiting for transfers between devices: 165 us -> none  [the longest x1 132 us: per_device(): lax.psum(partial_grad / normalizer / grad_root, ('tm', 'batch'))]
    pallas_call x0 -> x1, Pallas kernels: none -> 62.3 us  [per_device(): pl.pallas_call(functools.partial(main_kernel, devices, batches, part), ou...]
    reduce_scatter x2 -> x0, waiting for transfers between devices: 57 us -> none  [the longest x1 33.1 us: per_device(): lax.psum_scatter(term_fake, 'tm', scatter_dimension=1, tiled=True)]
    dot_general x39 -> x2, matrix products: 53.1 us -> 0.63 us  [per_device(): jnp.dot(own_wave[None], t.reshape(freq_rows, -1), preferred_element_type=...]
    all_gather x5 -> x0, blocking collectives: 45.5 us -> none  [the longest x1 12.4 us: per_device(): lax.all_gather(noisy_patch.astype(jnp.float32), 'tm', axis=1, tiled=True)]
    psum x2 -> x0, blocking collectives: 34.7 us -> none  [the longest x1 21.3 us: per_device(): modul_real, modul_fake = lax.psum((share_real, share_fake), 'tm')]
    another operation x2 -> x0, loops' own time: 7.68 us -> none  [attend(): pieces = lax.map(one_block, starts)]
    dynamic_slice x8 -> x0, local copies, waits for them, and re-layouts: 5.27 us -> none  [the longest x4 3.61 us: attend(): pieces = lax.map(one_block, starts)]
  transfers between devices with their start and end apart: 5 -> 0, of which waited for: 4 -> 0; matrix products, arithmetic and copies ran while one was open for 8% -> 0% of each run, Pallas kernels for 0% -> 0%
where the time goes in v2:
time: 74.2 us; the launch traced here: 73.9 us
  Pallas kernels  62.3 us (84%)
  local copies, waits for them, and re-layouts  5.29 us (7%)
  matrix products  3.37 us (5%)
  other arithmetic  1.46 us (2%)
  between operations  1.46 us (2%)
    pallas_call x1, Pallas kernels, per_device(): pl.pallas_call(functools.partial(main_kernel, devices, batches, part), ou...  62.3 us
    unnamed x6, local copies, waits for them, and re-layouts  3.85 us
    dot_general x1, matrix products, per_device(): lax.dot_general(gen_weight, hidden_states[0], (((1,), (1,)), ((), ())), p...  2.74 us

profile of v2, /device:TPU:1, one launch (start us, length us, event | category | flops | bytes accessed | tf_op | source)
XLA Modules:
  0.0 73.9 jit_solution(4692440468453206647)
XLA Ops:
  0.6 0.0 copy-start
  1.4 0.1 sine_convert_fusion
  1.5 0.7 pad_maximum_fusion.1
  2.2 0.6 broadcast_in_dim.8.level_ref
  2.8 0.0 copy-start.1
  2.8 2.7 %fusion.6 = (bf16[64,128]{1,0:T(8,128)(2,1)}, bf16[64,128]{1,0:T(8,128)(2,1)}) fusion(bf16[1,64,128]{2,1,0:T(8,128)(2,1)} %param.22, f32[]{:T(128)S(6)} %div.10, f32[]{:T(128)S(6)} %sub.3, bf16[64,5120]{1,0:T(8,128)(2,1)} %param.21, bf16[1,128,5120]{2,1,0:T(8,128)(2,1)} %param.20), kind=kOutput, calls=%fused_computation.11 | convolution fusion | flops 83943424 | bytes 2015240 | tf_op jit(solution)/shard_map/dot_general | solution.py:372
  5.5 0.0 copy-done
  5.5 0.3 fusion
  5.9 0.0 copy-done.1
  5.9 0.3 fusion.3
  6.2 0.7 pad_maximum_fusion
  6.9 0.8 %copy.30.gain_ref = f32[2,128,2]{2,1,0:T(8,128)} copy(f32[2,128,2]{1,2,0:T(2,128)S(1)} %pad_maximum_fusion.1) | data formatting | bytes 4096 | tf_op jit(solution)/shard_map/stack | solution.py:454
  7.7 62.3 %shard_map.203 = (f32[64,128]{1,0:T(8,128)}, f32[64,5120]{1,0:T(8,128)}) custom-call(f32[8,128]{1,0:T(8,128)} %broadcast_in_dim.8.level_ref, bf16[64,128]{1,0:T(8,128)(2,1)} %get-tuple-element.6.noisy_ref, bf16[64,128]{1,0:T(8,128)(2,1)} %get-tuple-element.7.made_ref, f32[8,6,640]{2,1,0:T(8,128)} %bitcast.64, f32[2,128,2]{2,1,0:T(8,128)} %copy.30.gain_ref, ...), custom_call_target="tpu_custom_call" | custom-call | tf_op jit(solution)/shard_map/pallas_call | solution.py:437
  70.0 1.4 %copy.60 = f32[1,64,128]{2,1,0:T(8,128)} copy(f32[1,64,128]{2,1,0:T(8,128)} %bitcast.67) | data formatting | bytes 65536
  71.4 2.5 %copy.61 = f32[64,5120]{1,0:T(8,128)} copy(f32[64,5120]{1,0:T(8,128)} %get-tuple-element.13) | data formatting | bytes 2621440
  (3 shorter events, 0.1 us)
Async XLA Ops:
  0.6 4.9 %copy-start = (bf16[32,3,5120]{2,0,1:T(8,128)(2,1)S(1)}, bf16[32,3,5120]{2,0,1:T(8,128)(2,1)}, u32[]{:S(2)}) copy-start(bf16[32,3,5120]{2,0,1:T(8,128)(2,1)} %param.33) | copy-start | bytes 2949124
  2.8 3.1 %copy-start.1 = (bf16[32,3,5120]{2,0,1:T(8,128)(2,1)S(1)}, bf16[32,3,5120]{2,0,1:T(8,128)(2,1)}, u32[]{:S(2)}) copy-start(bf16[32,3,5120]{2,0,1:T(8,128)(2,1)} %param.25) | copy-start | bytes 2949124

commit v3 on v2

--- a/solution.py
+++ b/solution.py
@@ -23,17 +23,19 @@
 bf16 = jnp.bfloat16
 
 
-def greet(sizes):
+def hail(sizes):
     barrier = pltpu.get_barrier_semaphore()
-    count = 0
     for axis, size in sizes.items():
         me = lax.axis_index(axis)
         for k in range(1, size):
             pl.semaphore_signal(
                 barrier, inc=1, device_id={axis: lax.rem(me + k, size)}, device_id_type=MESH
             )
-            count += 1
-    pl.semaphore_wait(barrier, count)
+
+
+def meet(sizes):
+    count = sum(size - 1 for size in sizes.values())
+    pl.semaphore_wait(pltpu.get_barrier_semaphore(), count)
 
 
 def exchange(axis, size, source, slots, send, recv):
@@ -81,31 +83,49 @@
     return jnp.dot(left, right, preferred_element_type=f32)
 
 
-def main_kernel(n, nb, part, level_ref, noisy_ref, made_ref, share_ref, gain_ref, *refs):
-    big, refs = refs[:13], refs[13:]
-    (dmd_ref, weight_ref), refs = refs[:2], refs[2:]
-    held, refs = refs[:13], refs[13:]
+def main_kernel(n, nb, part, level_ref, wave_ref, noise_ref, gain_real, gain_fake, *refs):
+    big, refs = refs[:16], refs[16:]
+    (difference_ref, norm_ref, weight_ref), refs = refs[:3], refs[3:]
+    held, refs = refs[:16], refs[16:]
     (load_sem, patches, parts, modul, fold, gate_fold, gram, inner, stack, qkv, squares,
-     square_parts, keys, terms, term_parts, gap, gaps, halves, partner, across_chips, reduced,
-     chip_parts, mixed, quarters, merged, grad) = refs[:26]
+     square_parts, keys, terms, term_parts, gap, gaps, noisy_ref, share_ref, columns_held, rounded,
+     all_rounded, mixed, quarters, merged, grad) = refs[:26]
     sem = refs[26:]
     me = lax.axis_index("tm")
     mine = lax.axis_index("batch")
     core, chip = lax.rem(me, 2), lax.div(me, 2)
     chips = n // 2
     patch_rows, frame = noisy_ref.shape
+    level = level_ref[0, 0]
     tokens = n * frame
     width = held[0].shape[1]
     chunks = width // part
     loads = []
     for i, (source, target) in enumerate(zip(big, held)):
-        load = pltpu.make_async_copy(source, target, load_sem.at[i])
-        load.start()
-        loads.append(load)
+        loads.append(pltpu.make_async_copy(source, target, load_sem.at[i]))
+    for i in (13, 12, 14, 15, *range(12)):
+        loads[i].start()
     nets = [held[6 * i : 6 * i + 6] for i in (0, 1)]
     hidden = held[12]
 
-    greet({"tm": n, "batch": nb})
+    hail({"tm": n, "batch": nb})
+    loads[13].wait()
+    loads[12].wait()
+    made = dot_nt(held[13][...], hidden[...]).astype(bf16).astype(f32)
+    noisy = ((1.0 - level) * made + level * noise_ref[...].astype(f32)).astype(bf16)
+    noisy_ref[...] = noisy
+    noisy = noisy.astype(f32)
+    for i in (0, 1):
+        loads[14 + i].wait()
+        for j in range(3):
+            share = dot(wave_ref[...], held[14 + i][j])
+            for s in range(n):
+                if s < chunks:
+                    row = share[:1, s * part : (s + 1) * part]
+                else:
+                    row = jnp.zeros((1, part), f32)
+                share_ref[s, 3 * i + j : 3 * i + j + 1] = row
+    meet({"tm": n, "batch": nb})
     scatter = exchange("tm", n, lambda peer: share_ref.at[peer], parts, sem[0], sem[1])
     spread = exchange("tm", n, lambda peer: noisy_ref, patches, sem[2], sem[3])
     parts[me] = share_ref[me]
@@ -116,6 +136,12 @@
 
     def columns(s):
         return pl.ds(pl.multiple_of(s * part, 128), part)
+
+    def own_columns(peer):
+        return hidden.at[:, columns(lax.rem(peer, chunks))]
+
+    pass_hidden = exchange("tm", n, own_columns, columns_held, sem[10], sem[11])
+    columns_held[me] = hidden[:, columns(lax.rem(me, chunks))]
 
     means = []
     for i, (embed, proj, query, key, value, out) in enumerate(nets):
@@ -193,14 +219,14 @@
 
     block = 2 * frame
     groups = min(4, tokens // block)
+    gains = [ref[0:1, :] * ref[1:2, :] for ref in (gain_real, gain_fake)]
     per_group = tokens // block // groups
     for i in range(2):
         for s in range(n):
             at = slice(s * frame, (s + 1) * frame)
             gained = qkv[i, head : 2 * head, at] * inverse[2 * i + 1 : 2 * i + 2, at]
-            keys[i, at, :] = (gained * gain_ref[i, :, 1:2]).T.astype(bf16)
-            gained = qkv[i, :head, at] * inverse[2 * i : 2 * i + 1, at]
-            qkv[i, :head, at] = gained * gain_ref[i, :, 0:1]
+            keys[i, at, :] = (gained.T * gains[i]).astype(bf16)
+            qkv[i, :head, at] = qkv[i, :head, at] * inverse[2 * i : 2 * i + 1, at]
     fold_outs = [
         (gate_fold[i, :patch_rows] + gate_fold[i, patch_rows:]).astype(bf16) for i in range(2)
     ]
@@ -243,48 +269,48 @@
     term_parts[me] = terms[me]
     own = stack[:, pl.ds(pl.multiple_of(me * frame, frame), frame)]
     direct = [dot(jnp.concatenate(split(inner[i]), axis=1), own) for i in range(2)]
-    noisy = noisy_ref[...].astype(f32)
-    level = level_ref[:1, :1]
     landed(give)
     summed = jnp.sum(term_parts[...].astype(f32), axis=0)
     pred_real = noisy - level * (summed[:patch_rows] + direct[0])
     pred_fake = noisy - level * (summed[patch_rows:] + direct[1])
     difference = pred_fake - pred_real
-    distance = jnp.abs(made_ref[...].astype(f32) - pred_real)
+    distance = jnp.abs(made - pred_real)
     distance = jnp.sum(jnp.sum(distance, axis=0, keepdims=True), axis=1, keepdims=True)
     gap[...] = jnp.broadcast_to(distance, gap.shape)
-    gap_copies = exchange("tm", n, lambda peer: gap, gaps, sem[10], sem[11])
+    rounded[...] = difference.astype(bf16)
+    difference_copies = exchange("tm", n, lambda peer: rounded, all_rounded, sem[12], sem[13])
+    gap_copies = exchange("tm", n, lambda peer: gap, gaps, sem[14], sem[15])
     gaps[me] = gap[...]
-    loads[12].wait()
-    rounded = difference.astype(bf16)
-    for s in range(n):
-        if s < chunks:
-            piece = dot(rounded, hidden[:, s * part : (s + 1) * part]).astype(bf16)
-        else:
-            piece = jnp.zeros(halves.shape[2:], bf16)
-        halves[s % 2, s // 2] = piece
-    swap = pltpu.make_async_remote_copy(
-        src_ref=halves.at[1 - core],
-        dst_ref=partner,
-        send_sem=sem[12].at[0],
-        recv_sem=sem[12].at[1],
-        device_id={"tm": me + 1 - 2 * core},
-        device_id_type=MESH,
-    )
-    swap.start()
-    swap.wait_recv()
-    for k in range(chips):
-        reduced[k] = (halves[core, k].astype(f32) + partner[k].astype(f32)).astype(bf16)
-
-    def between_chips(source, slots, send, recv):
+    all_rounded[me] = rounded[...]
+    difference_ref[...] = difference
+    landed(pass_hidden)
+    landed(difference_copies)
+    total = dot(all_rounded[0], columns_held[0])
+    for s in range(1, n):
+        total = total + dot(all_rounded[s], columns_held[s])
+    landed(gap_copies)
+    normalizer = jnp.maximum(jnp.sum(gaps[...], axis=0) / (patch_rows * tokens), gap_floor)
+    norm_ref[...] = normalizer
+    total = total / normalizer[:1, :1] / math.sqrt(nb * tokens)
+    mixed[...] = total.reshape(mixed.shape).astype(bf16)
+    across = exchange("batch", nb, lambda peer: mixed.at[peer], quarters, sem[16], sem[17])
+    quarters[mine] = mixed[mine]
+    landed(across)
+    merged[mine] = jnp.sum(quarters[...].astype(f32), axis=0).astype(bf16)
+    back = exchange("batch", nb, lambda peer: merged.at[mine], merged, sem[18], sem[19])
+
+    grad[core, chip, mine] = merged[mine]
+    chain = []
+
+    def to_chips(piece, k):
         copies = []
-        for k in range(1, chips):
-            peer = lax.rem(chip + k, chips)
+        for hop in range(1, chips):
+            peer = lax.rem(chip + hop, chips)
             copy = pltpu.make_async_remote_copy(
-                src_ref=source(peer),
-                dst_ref=slots(chip),
-                send_sem=send.at[k],
-                recv_sem=recv.at[k],
+                src_ref=merged.at[piece],
+                dst_ref=grad.at[core, chip, piece],
+                send_sem=sem[20].at[k * chips + hop],
+                recv_sem=sem[21].at[k * chips + hop],
                 device_id={"tm": 2 * peer + core},
                 device_id_type=MESH,
             )
@@ -292,43 +318,37 @@
             copies.append(copy)
         return copies
 
-    chip_copies = between_chips(
-        lambda peer: reduced.at[peer], lambda at: chip_parts.at[at], sem[13], sem[14]
-    )
-    chip_parts[chip] = reduced[chip]
-    landed(gap_copies)
-    normalizer = jnp.maximum(jnp.sum(gaps[...], axis=0) / (patch_rows * tokens), gap_floor)[:1, :1]
-    dmd_ref[...] = difference / normalizer
-    landed(chip_copies)
-    grad_root = math.sqrt(nb * tokens)
-    total = jnp.sum(chip_parts[...].astype(f32), axis=0) / normalizer / grad_root
-    mixed[...] = total.reshape(mixed.shape).astype(bf16)
-    across = exchange("batch", nb, lambda peer: mixed.at[peer], quarters, sem[15], sem[16])
-    quarters[mine] = mixed[mine]
-    landed(across)
-    merged[mine] = jnp.sum(quarters[...].astype(f32), axis=0).astype(bf16)
-    back = exchange("batch", nb, lambda peer: merged.at[mine], merged, sem[17], sem[18])
-    landed(back)
-    grad[core, chip] = merged[...]
-    last = between_chips(lambda peer: merged, lambda at: grad.at[core, at], sem[19], sem[20])
-    landed(last)
-    share = pltpu.make_async_remote_copy(
-        src_ref=grad.at[core],
-        dst_ref=grad.at[core],
-        send_sem=sem[12].at[2],
-        recv_sem=sem[12].at[3],
-        device_id={"tm": me + 1 - 2 * core},
-        device_id_type=MESH,
-    )
-    share.start()
-    share.wait_recv()
+    chain.append(to_chips(mine, 0))
+    for k in range(1, nb):
+        back[k - 1].wait_recv()
+        piece = lax.rem(mine + nb - k, nb)
+        grad[core, chip, piece] = merged[piece]
+        chain.append(to_chips(piece, k))
+
+    def to_partner(at, hop):
+        copy = pltpu.make_async_remote_copy(
+            src_ref=grad.at[core, at],
+            dst_ref=grad.at[core, at],
+            send_sem=sem[22].at[hop],
+            recv_sem=sem[23].at[hop],
+            device_id={"tm": me + 1 - 2 * core},
+            device_id_type=MESH,
+        )
+        copy.start()
+        return copy
+
+    shares = [to_partner(chip, 0)]
+    for hop in range(1, chips):
+        for copies in chain:
+            copies[hop - 1].wait_recv()
+        shares.append(to_partner(lax.rem(chip + chips - hop, chips), hop))
+    landed(shares)
     for s in range(chunks):
-        piece = grad[s % 2, s // 2].astype(f32)
+        piece = grad[s % 2, s // 2]
         weight_ref[:, s * part : (s + 1) * part] = piece.reshape(patch_rows, part)
-    swap.wait_send()
-    share.wait_send()
     for copies in (
-        scatter, spread, collect, sums, give, gap_copies, chip_copies, across, back, last
+        scatter, spread, collect, pass_hidden, sums, give, difference_copies, gap_copies,
+        across, back, *chain, shares,
     ):
         gone(copies)
 
@@ -369,12 +389,6 @@
     time_step = timesteps[0]
     level_raw = time_step.astype(jnp.float32) / 1000.0
     noise_level = 5.0 * level_raw / (1.0 + 4.0 * level_raw)
-    generated = lax.dot_general(
-        gen_weight, hidden_states[0], (((1,), (1,)), ((), ())), preferred_element_type=f32
-    ).astype(bf16)
-    noisy_patch = (
-        (1.0 - noise_level) * generated.astype(f32) + noise_level * noise_field[0].astype(f32)
-    ).astype(bf16)
     sinus_wave = sinusoid(time_step)
     freq_rows = time_real.shape[0]
     own_wave = lax.dynamic_slice_in_dim(sinus_wave, lax.axis_index("tm") * freq_rows, freq_rows, 0)
@@ -383,22 +397,13 @@
     part = -(-model_width // (devices * 128)) * 128
     while model_width % part:
         part += 128
-    padding = ((0, 0), (0, devices * part - model_width))
-    shares = jnp.concatenate(
-        [
-            jnp.dot(own_wave[None], t.reshape(freq_rows, -1), preferred_element_type=f32).reshape(
-                3, model_width
-            )
-            for t in (time_real, time_fake)
-        ]
-    )
-    shares = jnp.pad(shares, padding).reshape(6, devices, part).transpose(1, 0, 2)
     n, chips, quarter, head = devices, devices // 2, patch_rows // batches, query_real.shape[1]
     kin = 2 * patch_rows
     big = (
         embed_real, proj_real, query_real, key_real, value_real, out_real,
         embed_fake, proj_fake, query_fake, key_fake, value_fake, out_fake,
-        hidden_states[0],
+        hidden_states[0], gen_weight,
+        time_real.transpose(1, 0, 2), time_fake.transpose(1, 0, 2),
     )
     vm = pltpu.VMEM
     scratch = [
@@ -420,41 +425,40 @@
         vm((n, kin, frame_tokens), bf16),
         vm((8, 128), f32),
         vm((n, 8, 128), f32),
-        vm((2, chips, patch_rows, part), bf16),
-        vm((chips, patch_rows, part), bf16),
-        vm((8, 128), f32),
-        vm((chips, patch_rows, part), bf16),
-        vm((chips, patch_rows, part), bf16),
+        vm((patch_rows, frame_tokens), bf16),
+        vm((n, 6, part), f32),
+        vm((n, frame_tokens, part), bf16),
+        vm((patch_rows, frame_tokens), bf16),
+        vm((n, patch_rows, frame_tokens), bf16),
         vm((batches, quarter, part), bf16),
         vm((batches, quarter, part), bf16),
         vm((batches, quarter, part), bf16),
         vm((2, chips, batches, quarter, part), bf16),
-        *sems(n, n, n, n, n, n),
-        pltpu.SemaphoreType.DMA((4,)),
-        *sems(chips, batches, batches, chips),
+        *sems(n, n, n, n, n, n, n, n, batches, batches, batches * chips, chips),
     ]
     vmem = pl.BlockSpec(memory_space=pltpu.VMEM)
-    dmd, weight_grad = pl.pallas_call(
+    difference, norm, weight_grad = pl.pallas_call(
         functools.partial(main_kernel, devices, batches, part),
         out_shape=[
             jax.ShapeDtypeStruct((patch_rows, frame_tokens), f32),
-            jax.ShapeDtypeStruct((patch_rows, model_width), f32),
+            jax.ShapeDtypeStruct((8, 128), f32),
+            jax.ShapeDtypeStruct((patch_rows, model_width), bf16),
         ],
-        in_specs=[vmem] * 5 + [pl.BlockSpec(memory_space=pl.ANY)] * len(big),
-        out_specs=[vmem, vmem],
+        in_specs=[pl.BlockSpec(memory_space=pltpu.SMEM)] + [vmem] * 4 + [pl.BlockSpec(memory_space=pl.ANY)] * len(big),
+        out_specs=[vmem] * 3,
         scratch_shapes=scratch,
         compiler_params=pltpu.CompilerParams(
             collective_id=0, has_side_effects=True, vmem_limit_bytes=60 * 1024 * 1024
         ),
     )(
-        jnp.broadcast_to(noise_level, (8, 128)),
-        noisy_patch,
-        generated,
-        shares,
-        jnp.stack([gain_real.T, gain_fake.T]),
+        noise_level.reshape(1, 1),
+        jnp.broadcast_to(own_wave, (16, freq_rows)),
+        noise_field[0],
+        gain_real,
+        gain_fake,
         *big,
     )
-    return (dmd[None], weight_grad)
+    return ((difference / norm[0, 0])[None], weight_grad.astype(f32))
 
 
 def solution(mesh):

time: 74.2 us -> 69.9 us (0.942)
  local copies, waits for them, and re-layouts: 5.29 us -> 1.87 us
  matrix products: 3.37 us -> 0 us
  other arithmetic: 1.46 us -> 4.31 us
    unnamed x6 -> x0, local copies, waits for them, and re-layouts: 3.85 us -> none
    dot_general x3 -> x0, matrix products: 3.37 us -> none  [the longest x1 2.74 us: per_device(): lax.dot_general(gen_weight, hidden_states[0], (((1,), (1,)), ((), ())), p...]
    convert_element_type x0 -> x1, other arithmetic: none -> 2.23 us  [per_device(): return ((difference / norm[0, 0])[None], weight_grad.astype(f32))]
    broadcast_in_dim x0 -> x1, other arithmetic: none -> 2.03 us  [per_device(): return ((difference / norm[0, 0])[None], weight_grad.astype(f32))]
    slice x0 -> x1, local copies, waits for them, and re-layouts: none -> 1.19 us  [per_device(): return ((difference / norm[0, 0])[None], weight_grad.astype(f32))]
    another operation x1 -> x0, local copies, waits for them, and re-layouts: 0.8 us -> none  [per_device(): jnp.stack([gain_real.T, gain_fake.T])]
where the time goes in v3:
time: 69.9 us; the launch traced here: 69.5 us
  Pallas kernels  62 us (89%)
  other arithmetic  4.31 us (6%)
  local copies, waits for them, and re-layouts  1.87 us (3%)
  between operations  1.34 us (2%)
    pallas_call x1, Pallas kernels, per_device(): pl.pallas_call(functools.partial(main_kernel, devices, batches, part), ou...  62 us
    convert_element_type x1, other arithmetic, per_device(): return ((difference / norm[0, 0])[None], weight_grad.astype(f32))  2.23 us
    broadcast_in_dim x1, other arithmetic, per_device(): return ((difference / norm[0, 0])[None], weight_grad.astype(f32))  2.03 us

profile of v3, /device:TPU:1, one launch (start us, length us, event | category | flops | bytes accessed | tf_op | source)
XLA Modules:
  0.0 69.5 jit_solution(9663553501627468806)
XLA Ops:
  1.3 0.1 sine_convert_fusion
  1.4 0.1 dynamic_slice.3
  1.5 0.6 broadcast_in_dim.6.wave_ref
  2.1 62.0 %shard_map.203 = (f32[64,128]{1,0:T(8,128)}, f32[8,128]{1,0:T(8,128)}, bf16[64,5120]{1,0:T(8,128)(2,1)}) custom-call(f32[1,1]{1,0:T(1,128)} %bitcast.1.level_ref, bf16[16,32]{1,0:T(8,128)(2,1)} %broadcast_in_dim.6.wave_ref, bf16[64,128]{1,0:T(8,128)(2,1)} %bitcast.12, f32[2,128]{1,0:T(2,128)} %gain_real.1, f32[2,128]{1,0:T(2,128)} %gain_fake.1, ...), custom_call_target="tpu_custom_call" | custom-call | tf_op jit(solution)/shard_map/pallas_call | solution.py:440
  64.1 1.2 %slice.3 = f32[1,1]{1,0:T(1,128)} slice(f32[8,128]{1,0:T(8,128)} %get-tuple-element.6), slice={[0:1], [0:1]} | slice | bytes 8 | tf_op jit(solution)/shard_map/slice | solution.py:461
  65.3 2.0 %divide_bitcast_fusion = f32[1,64,128]{2,1,0:T(8,128)} fusion(f32[64,128]{1,0:T(8,128)} %get-tuple-element.5, f32[]{:T(128)} %bitcast.6), kind=kLoop, calls=%fused_computation | loop fusion | flops 8192 | bytes 65540 | tf_op jit(solution)/shard_map/broadcast_in_dim | solution.py:461
  67.3 2.2 %convert_element_type.13 = f32[64,5120]{1,0:T(8,128)} convert(bf16[64,5120]{1,0:T(8,128)(2,1)} %get-tuple-element.7) | non-fusion elementwise | flops 327680 | bytes 1966080 | tf_op jit(solution)/shard_map/convert_element_type | solution.py:461
  (1 shorter events, 0.0 us)

commit v4 on v3

--- a/solution.py
+++ b/solution.py
@@ -282,7 +282,6 @@
     gap_copies = exchange("tm", n, lambda peer: gap, gaps, sem[14], sem[15])
     gaps[me] = gap[...]
     all_rounded[me] = rounded[...]
-    difference_ref[...] = difference
     landed(pass_hidden)
     landed(difference_copies)
     total = dot(all_rounded[0], columns_held[0])
@@ -291,6 +290,7 @@
     landed(gap_copies)
     normalizer = jnp.maximum(jnp.sum(gaps[...], axis=0) / (patch_rows * tokens), gap_floor)
     norm_ref[...] = normalizer
+    difference_ref[...] = difference / normalizer[:1, :1]
     total = total / normalizer[:1, :1] / math.sqrt(nb * tokens)
     mixed[...] = total.reshape(mixed.shape).astype(bf16)
     across = exchange("batch", nb, lambda peer: mixed.at[peer], quarters, sem[16], sem[17])
@@ -458,7 +458,7 @@
         gain_fake,
         *big,
     )
-    return ((difference / norm[0, 0])[None], weight_grad.astype(f32))
+    return (difference[None], weight_grad.astype(f32))
 
 
 def solution(mesh):

time: 69.9 us -> 67.2 us (0.961)
  other arithmetic: 4.31 us -> 2.29 us
    broadcast_in_dim x1 -> x0, other arithmetic: 2.03 us -> none  [per_device(): return ((difference / norm[0, 0])[None], weight_grad.astype(f32))]
    slice x1 -> x0, local copies, waits for them, and re-layouts: 1.19 us -> none  [per_device(): return ((difference / norm[0, 0])[None], weight_grad.astype(f32))]
where the time goes in v4:
time: 67.2 us; the launch traced here: 67 us
  Pallas kernels  62 us (92%)
  other arithmetic  2.29 us (3%)
  between operations  1.35 us (2%)
  local copies, waits for them, and re-layouts  1.3 us (2%)
    pallas_call x1, Pallas kernels, per_device(): pl.pallas_call(functools.partial(main_kernel, devices, batches, part), ou...  62 us
    convert_element_type x1, other arithmetic, per_device(): return (difference[None], weight_grad.astype(f32))  2.23 us

profile of v4, /device:TPU:1, one launch (start us, length us, event | category | flops | bytes accessed | tf_op | source)
XLA Modules:
  0.0 67.0 jit_solution(16807742316200290216)
XLA Ops:
  1.3 0.1 sine_convert_fusion
  1.4 0.1 dynamic_slice.3
  1.5 0.6 broadcast_in_dim.6.wave_ref
  2.1 62.0 %shard_map.203 = (f32[64,128]{1,0:T(8,128)}, f32[8,128]{1,0:T(8,128)}, bf16[64,5120]{1,0:T(8,128)(2,1)}) custom-call(f32[1,1]{1,0:T(1,128)} %bitcast.1.level_ref, bf16[16,32]{1,0:T(8,128)(2,1)} %broadcast_in_dim.6.wave_ref, bf16[64,128]{1,0:T(8,128)(2,1)} %bitcast.11, f32[2,128]{1,0:T(2,128)} %gain_real.1, f32[2,128]{1,0:T(2,128)} %gain_fake.1, ...), custom_call_target="tpu_custom_call" | custom-call | tf_op jit(solution)/shard_map/pallas_call | solution.py:440
  64.1 0.0 copy-start
  64.1 2.2 %convert_element_type.13 = f32[64,5120]{1,0:T(8,128)} convert(bf16[64,5120]{1,0:T(8,128)(2,1)} %get-tuple-element.5) | non-fusion elementwise | flops 327680 | bytes 1966080 | tf_op jit(solution)/shard_map/convert_element_type | solution.py:461
  66.3 0.0 copy-done
  66.3 0.6 copy.24
  (1 shorter events, 0.0 us)
Async XLA Ops:
  64.1 2.2 %copy-start = (f32[64,128]{1,0:T(8,128)S(1)}, f32[64,128]{1,0:T(8,128)}, u32[]{:S(2)}) copy-start(f32[64,128]{1,0:T(8,128)} %get-tuple-element.4) | copy-start | bytes 98308
